TPU v7x, 512 devices: a whole 4x4x16 slice. The times are simulated.
512 devices in a mesh: leaf: 16 (over y_hi, x, core), ctx: 32 (over z, y_lo).
Axes of the slice: x: 4, y: 4 (y_hi: 2, y_lo: 2; y = y_hi * 2 + y_lo), z: 16, core: 2. Of those that a mesh axis runs over, the one named last changes fastest.
Arguments:
- queries: bfloat16 [65536, 4096], P(('leaf', 'ctx')), parts along dimension 0, may hold values from -6 to 6
- keys: bfloat16 [65536, 512], P(('leaf', 'ctx')), parts along dimension 0, may hold values from -6 to 6
- values: bfloat16 [65536, 512], P(('leaf', 'ctx')), parts along dimension 0, may hold values from -6 to 6
- grad_out: bfloat16 [65536, 4096], P(('leaf', 'ctx')), parts along dimension 0, may hold values from -6 to 6
- block_path: int32 [512, 4], P('leaf'), parts along dimension 0, may hold values from -1 to 31, as said below
- assistant: int32 [65536], P(('leaf', 'ctx')), parts along dimension 0, may hold values from 0 to 1, as said below
Outputs:
- attention: bfloat16 [65536, 4096], P(('leaf', 'ctx')), parts along dimension 0
- grad_queries: bfloat16 [65536, 4096], P(('leaf', 'ctx')), parts along dimension 0
- grad_keys: bfloat16 [65536, 512], P(('leaf', 'ctx')), parts along dimension 0
- grad_values: bfloat16 [65536, 512], P(('leaf', 'ctx')), parts along dimension 0
There are 16 independent parts, one for each index of `leaf`. A program takes and returns all parts, laid end to end along the dimension named above; each array names one. Nothing has to cross between parts.
Inputs may be any that keep to these rules, and one draw needn't show every extreme that they name: `block_path`: blocks lie in depth-first order of the tree; every node spans one block; block 0 is the root at depth 0. Row b holds at depth e <= depth(b) the block of b's ancestor node at that depth (b itself at e = depth(b)) and -1 below. `assistant`: each block of 128 tokens holds one run of ones.
All inputs are finite; a program needn't handle non-finite values.
Results may differ from a plain program's by a relative error of at most 0.0091.
Values may be sent and summed in bfloat16 or wider, within the bound.
A program may use at most 128 MiB of HBM per device.

v0:
```python
import math

import jax
import jax.numpy as jnp
from jax import lax
from jax.sharding import Mesh
from jax.sharding import PartitionSpec as P

KEY_HEADS = 4
HEAD_WIDTH = 128
HEADS_PER_KEY = 8
CTX = ("ctx_0", "ctx_1")
LEAF_CTX = ("leaf", "ctx_0", "ctx_1")


def sent_together(arrays, axis, dim, along):
    both = jnp.concatenate(arrays, axis=along)
    filled, at, done = (lax.all_gather(both, axis, axis=dim, tiled=True), 0, [])
    for a in arrays:
        done.append(lax.slice_in_dim(filled, at, at + a.shape[along], axis=along))
        at += a.shape[along]
    return tuple(done)


def nothing_yet(x, identity):
    return jax.tree.map(
        lambda a, e: jnp.broadcast_to(jnp.asarray(e, a.dtype), a.shape), x, identity
    )


def entering(x, axes, combine, identity):
    before = start = nothing_yet(x, identity)
    so_far = x
    for axis in reversed(axes):
        size, here = (lax.axis_size(axis), lax.axis_index(axis))
        pieces = jax.tree.map(lambda part: lax.all_gather(part, axis), so_far)
        inside, so_far = (start, start)
        for k in reversed(range(size)):
            passed = k > here
            so_far = combine(so_far, jax.tree.map(lambda part: part[k], pieces))
            inside = jax.tree.map(lambda new, old: jnp.where(passed, new, old), so_far, inside)
        before = combine(inside, before)
    return before


def dot_rows(left, right):
    return lax.dot_general(
        left, right, (((1,), (1,)), ((), ())), preferred_element_type=jnp.float32
    )


def dot_cols(left, right):
    return lax.dot_general(
        left, right, (((0,), (0,)), ((), ())), preferred_element_type=jnp.float32
    )


def attend_block(queries, grad_rows, slot_keys, slot_values, allowed):
    block_rows = queries.shape[0]
    head_cols = HEADS_PER_KEY * HEAD_WIDTH
    scaling = 1.0 / math.sqrt(HEAD_WIDTH)
    wide_mask = jnp.repeat(allowed, HEADS_PER_KEY, axis=0)
    attended_parts, query_parts, key_parts, value_parts = ([], [], [], [])
    for key_value_head in range(KEY_HEADS):
        query_matrix = queries[
            :, key_value_head * head_cols : (key_value_head + 1) * head_cols
        ].reshape(block_rows * HEADS_PER_KEY, HEAD_WIDTH)
        grad_head = grad_rows[
            :, key_value_head * head_cols : (key_value_head + 1) * head_cols
        ].reshape(block_rows * HEADS_PER_KEY, HEAD_WIDTH)
        key_cols = slot_keys[:, key_value_head * HEAD_WIDTH : (key_value_head + 1) * HEAD_WIDTH]
        value_cols = slot_values[:, key_value_head * HEAD_WIDTH : (key_value_head + 1) * HEAD_WIDTH]
        scores = jnp.where(wide_mask, dot_rows(query_matrix, key_cols) * scaling, -jnp.inf)
        row_max = jnp.max(scores, axis=1, keepdims=True)
        row_sum = jnp.sum(jnp.exp(scores - row_max), axis=1, keepdims=True)
        log_total = row_max + jnp.log(row_sum)
        rounded = jnp.exp(scores - log_total).astype(jnp.bfloat16)
        attended = jnp.dot(rounded, value_cols, preferred_element_type=jnp.float32).astype(
            jnp.bfloat16
        )
        attended = lax.optimization_barrier(attended)
        row_delta = jnp.sum(
            grad_head.astype(jnp.float32) * attended.astype(jnp.float32), axis=1, keepdims=True
        )
        grad_prob = dot_rows(grad_head, value_cols)
        grad_score = (jnp.exp(scores - log_total) * (grad_prob - row_delta)).astype(jnp.bfloat16)
        grad_query = (
            jnp.dot(grad_score, key_cols, preferred_element_type=jnp.float32) * scaling
        ).astype(jnp.bfloat16)
        grad_key = dot_cols(grad_score, query_matrix) * scaling
        grad_value = dot_cols(rounded, grad_head)
        attended_parts.append(attended.reshape(block_rows, head_cols))
        query_parts.append(grad_query.reshape(block_rows, head_cols))
        key_parts.append(grad_key)
        value_parts.append(grad_value)
    return (
        jnp.concatenate(attended_parts, 1),
        jnp.concatenate(query_parts, 1),
        jnp.concatenate(key_parts, 1),
        jnp.concatenate(value_parts, 1),
    )


def on_device(queries, keys, values, grad_out, block_path, assistant):
    block_rows = queries.shape[0]
    kv_width = keys.shape[1]
    position = lax.axis_index(CTX)
    depths = jnp.sum((block_path >= 0).astype(jnp.int32), axis=1) - 1
    own_path = lax.dynamic_index_in_dim(block_path, position, 0, keepdims=False)
    own_depth = lax.dynamic_index_in_dim(depths, position, 0, keepdims=False)
    seen_slots = jnp.stack([own_depth > 0, own_depth > 1, own_depth > 2])
    wanted_blocks = jnp.stack([own_path[0], own_path[1], own_path[2]])
    row_ids = jnp.arange(block_rows, dtype=jnp.int32)
    empty = jnp.zeros((3, block_rows, kv_width), jnp.bfloat16)
    picked = (empty, empty)
    key_piece, value_piece = sent_together((keys, values), CTX, 0, 1)
    piece_rows = key_piece.shape[0]
    for slot_number in range(3):
        wanted = wanted_blocks[slot_number]
        begin = wanted * block_rows
        touches = (wanted >= 0) & (begin < piece_rows) & (begin + block_rows > 0)

        def fill(current, slot_number=slot_number, begin=begin):
            local_rows = begin + row_ids
            inside = (local_rows >= 0) & (local_rows < piece_rows)
            clipped = jnp.clip(local_rows, 0, piece_rows - 1)
            new_keys = jnp.where(inside[:, None], key_piece[clipped], current[0][slot_number])
            new_values = jnp.where(inside[:, None], value_piece[clipped], current[1][slot_number])
            return (
                current[0].at[slot_number].set(new_keys),
                current[1].at[slot_number].set(new_values),
            )

        def unchanged(current):
            return current

        picked = lax.cond(touches, fill, unchanged, picked)
    far_keys, far_values = picked
    slot_keys = jnp.concatenate([far_keys.reshape(3 * block_rows, kv_width), keys], 0)
    slot_values = jnp.concatenate([far_values.reshape(3 * block_rows, kv_width), values], 0)
    full_slots = jnp.repeat(seen_slots, block_rows)
    causal = jnp.arange(block_rows)[:, None] >= jnp.arange(block_rows)[None, :]
    allowed = jnp.concatenate(
        [jnp.broadcast_to(full_slots[None, :], (block_rows, 3 * block_rows)), causal], 1
    )
    grad_rows = grad_out * assistant[:, None].astype(jnp.bfloat16)
    attention, grad_queries, grad_key_all, grad_value_all = attend_block(
        queries, grad_rows, slot_keys, slot_values, allowed
    )
    slot_grads = jnp.stack(
        [
            grad_key_all.reshape(4, block_rows, kv_width),
            grad_value_all.reshape(4, block_rows, kv_width),
        ],
        1,
    )
    grad_total = slot_grads[3]
    tree_depths = [0, 1, 2]
    resets = jnp.stack([own_depth <= tree_level for tree_level in tree_depths]).astype(jnp.float32)
    carried = jnp.stack([slot_grads[tree_level] for tree_level in tree_depths])

    def accumulate(earlier, latter):
        marker = jnp.maximum(earlier[0], latter[0])
        summed = jnp.where(latter[0][:, None, None, None] > 0.5, latter[1], earlier[1] + latter[1])
        return (marker, summed)

    identity = (jnp.zeros_like(resets), jnp.zeros_like(carried))
    _, received = entering((resets, carried), CTX, accumulate, identity)
    for slot_index, tree_level in enumerate(tree_depths):
        grad_total = grad_total + jnp.where(own_depth == tree_level, received[slot_index], 0.0)
    return (
        attention,
        grad_queries,
        grad_total[0].astype(jnp.bfloat16),
        grad_total[1].astype(jnp.bfloat16),
    )


def solution(mesh):
    split = Mesh(mesh.devices.reshape(mesh.shape["leaf"], 16, 2), ("leaf", "ctx_0", "ctx_1"))
    in_specs = (
        P(LEAF_CTX, None),
        P(LEAF_CTX, None),
        P(LEAF_CTX, None),
        P(LEAF_CTX, None),
        P("leaf", None),
        P(LEAF_CTX),
    )
    out_specs = (P(LEAF_CTX, None), P(LEAF_CTX, None), P(LEAF_CTX, None), P(LEAF_CTX, None))
    return jax.shard_map(
        on_device, mesh=split, in_specs=in_specs, out_specs=out_specs, check_vma=False
    )
```

profile of v0, /device:TPU:6, one launch (start us, length us, event | category | flops | bytes accessed | tf_op | source)
XLA Modules:
  0.0 614.2 jit_solution(16256079082961271909)
XLA Ops:
  7.2 1.8 pad_maximum_fusion.5
  20.6 1.9 reshape.634
  24.8 185.2 %all-gather.7.cloned.1.call-done = bf16[4096,1024]{1,0:T(8,128)(2,1)} async-done(((bf16[128,1024]{1,0:T(8,128)(2,1)}), bf16[4096,1024]{1,0:T(8,128)(2,1)}) %all-gather.7.cloned.1.call-update) | async-done | bytes 8388624 | tf_op jit(solution)/shard_map/all_gather | solution.py:18
  210.0 5.7 fusion.49
  215.7 7.4 %conditional.3 = (bf16[3,128,512]{2,1,0:T(8,128)(2,1)S(1)}, bf16[3,128,512]{2,1,0:T(8,128)(2,1)S(1)}) conditional(s32[]{:T(128)} %convert_element_type.109, () %tuple.66, (s32[]{:T(128)}, s32[128]{0:T(128)S(1)}, bf16[4096,512]{1,0:T(8,128)(2,1)}, bf16[4096,512]{1,0:T(8,128)(2,1)}) %tuple.67), branch_computations={%region_1.2_spmd, %region_2.3_spmd} | conditional | flops 133248 | bytes 2104604 | solution.py:137
  215.7 3.6 gather_fusion.1
  219.4 3.6 gather_fusion
  233.3 1.5 multiply_convert_fusion.2
  235.5 1.5 multiply_convert_fusion.3
  238.1 1.6 copy.41
  239.7 1.8 convolution_multiply_fusion.4
  241.5 1.4 convolution_multiply_fusion.5
  245.0 1.6 copy.40
  250.1 11.7 %all-gather.1 = f32[2,1,3]{2,1,0:T(1,128)S(1)} all-gather(f32[1,1,3]{2,1,0:T(1,128)S(1)} %fusion.48), channel_id=1, replica_groups=mesh['leaf'=16,'ctx_0'=16,'ctx_1'=2] {'ctx_1'}, dimensions={0}, use_global_device_ids=true | all-gather | bytes 36 | tf_op jit(solution)/shard_map/all_gather | solution.py:36
  261.8 54.9 %all-gather.11.cloned.1.call-done = f32[6,2,128,512]{3,2,1,0:T(8,128)} async-done(((f32[3,2,128,512]{3,2,1,0:T(8,128)}), f32[6,2,128,512]{3,2,1,0:T(8,128)}) %all-gather.11.cloned.1.call-update) | async-done | bytes 3145744 | tf_op jit(solution)/shard_map/all_gather | solution.py:36
  316.8 3.7 add_select_fusion.16
  322.6 30.7 %all-gather.2 = f32[16,1,3]{2,1,0:T(1,128)S(1)} all-gather(f32[1,1,3]{2,1,0:T(1,128)S(1)} %get-tuple-element.161), channel_id=1, replica_groups=mesh['leaf'=16,'ctx_0'=16,'ctx_1'=2] {'ctx_0'}, dimensions={0}, use_global_device_ids=true | all-gather | bytes 204 | tf_op jit(solution)/shard_map/all_gather | solution.py:36
  355.8 1.9 reshape.631
  357.7 1.4 fusion.13
  362.1 1.4 fusion.11
  366.6 2.3 pad_maximum_fusion.1
  368.9 2.3 pad_maximum_fusion.2
  371.2 224.9 %all-gather.9.cloned.1.call-done = f32[16,3,2,128,512]{4,3,2,1,0:T(8,128)} async-done(((f32[1,3,2,128,512]{4,3,2,1,0:T(8,128)}), f32[16,3,2,128,512]{4,3,2,1,0:T(8,128)}) %all-gather.9.cloned.1.call-update) | async-done | bytes 25165840 | tf_op jit(solution)/shard_map/all_gather | solution.py:36
  596.1 10.6 %add_select_fusion = f32[3,2,128,512]{3,2,1,0:T(8,128)S(1)} fusion(f32[16,3,2,128,512]{4,3,2,1,0:T(8,128)} %all-gather.9.cloned.1.call-done, f32[6,2,128,512]{3,2,1,0:T(8,128)S(1)} %copy-done, pred[3]{0:T(512)(128)(4,1)S(1)} %get-tuple-element.194, pred[3]{0:T(512)(128)(4,1)S(1)} %get-tuple-element.181, pred[3]{0:T(512)(128)(4,1)S(1)} %get-tuple-element.182, ...), kind=kLoop, calls=%fused_computation.25 | loop fusion | flops 20447232 | bytes 29884484 | tf_op jit(solution)/shard_map/jit(_where)/select_n | solution.py:164
  (147 shorter events, 33.0 us)
Async XLA Ops:
  7.2 11.4 %copy-start.24 = (bf16[128,4096]{1,0:T(8,128)(2,1)S(1)}, bf16[128,4096]{1,0:T(8,128)(2,1)}, u32[]{:S(2)}) copy-start(bf16[128,4096]{1,0:T(8,128)(2,1)} %param.24) | copy-start | bytes 3145732
  7.2 202.8 %all-gather.7.cloned.1.call-start = ((), (), s32[]{:S(2)}) async-start(), calls=%async_computation | async-start | bytes 8650752 | tf_op jit(solution)/shard_map/all_gather | solution.py:18
  9.0 307.7 %all-gather.11.cloned.1.call-start = ((), (), s32[]{:S(2)}) async-start(), calls=%async_computation.2 | async-start | bytes 4718592 | tf_op jit(solution)/shard_map/all_gather | solution.py:36
  18.6 5.5 copy-start.28
  18.6 5.5 copy-start.23
  20.6 203.5 %copy-start.17 = (bf16[1024,128]{1,0:T(8,128)(2,1)}, bf16[1024,128]{1,0:T(8,128)(2,1)S(1)}, u32[]{:S(2)}) copy-start(bf16[1024,128]{1,0:T(8,128)(2,1)S(1)} %reshape.636) | copy-start | bytes 786436
  224.1 4.5 copy-start.11
  227.2 4.6 copy-start.12
  228.7 4.4 copy-start.14
  230.1 5.3 copy-start.16
  232.6 8.9 %copy-start.5 = (bf16[1024,512]{0,1:T(8,128)(2,1)}, bf16[1024,512]{0,1:T(8,128)(2,1)S(1)}, u32[]{:S(2)}) copy-start(bf16[1024,512]{0,1:T(8,128)(2,1)S(1)} %multiply_convert_fusion.1) | copy-start | bytes 3145732
  239.7 6.9 %copy-start.1 = (f32[512,512]{1,0:T(8,128)}, f32[512,512]{1,0:T(8,128)S(1)}, u32[]{:S(2)}) copy-start(f32[512,512]{1,0:T(8,128)S(1)} %copy.41) | copy-start | bytes 3145732
  239.7 3.8 copy-start.9
  239.7 3.8 copy-start.22
  248.1 348.0 %all-gather.9.cloned.1.call-start = ((), (), s32[]{:S(2)}) async-start(), calls=%async_computation.1 | async-start | bytes 26738688 | tf_op jit(solution)/shard_map/all_gather | solution.py:36
  320.4 33.7 %copy-start.13 = (bf16[1024,128]{1,0:T(8,128)(2,1)S(1)}, bf16[1024,128]{1,0:T(8,128)(2,1)}, u32[]{:S(2)}) copy-start(bf16[1024,128]{1,0:T(8,128)(2,1)} %copy-done.12) | copy-start | bytes 786436
  320.4 34.6 %copy-start.15 = (bf16[1024,128]{1,0:T(8,128)(2,1)S(1)}, bf16[1024,128]{1,0:T(8,128)(2,1)}, u32[]{:S(2)}) copy-start(bf16[1024,128]{1,0:T(8,128)(2,1)} %copy-done.14) | copy-start | bytes 786436
  320.5 39.5 %copy-start.6 = (bf16[1024,512]{0,1:T(8,128)(2,1)S(1)}, bf16[1024,512]{0,1:T(8,128)(2,1)}, u32[]{:S(2)}) copy-start(bf16[1024,512]{0,1:T(8,128)(2,1)} %copy-done.5) | copy-start | bytes 3145732
  355.8 6.3 %copy-start.8 = (bf16[1024,512]{0,1:T(8,128)(2,1)S(1)}, bf16[1024,512]{0,1:T(8,128)(2,1)}, u32[]{:S(2)}) copy-start(bf16[1024,512]{0,1:T(8,128)(2,1)} %multiply_convert_fusion.2) | copy-start | bytes 3145732
  359.1 5.3 copy-start.10
  362.1 4.5 copy-start.25
  366.6 229.5 %copy-start = (f32[6,2,128,512]{3,2,1,0:T(8,128)S(1)}, f32[6,2,128,512]{3,2,1,0:T(8,128)}, u32[]{:S(2)}) copy-start(f32[6,2,128,512]{3,2,1,0:T(8,128)} %all-gather.11.cloned.1.call-done) | copy-start | bytes 9437188
  596.1 10.6 %copy-start.2 = (f32[512,512]{1,0:T(8,128)S(1)}, f32[512,512]{1,0:T(8,128)}, u32[]{:S(2)}) copy-start(f32[512,512]{1,0:T(8,128)} %copy-done.1) | copy-start | bytes 3145732
  596.1 10.6 %copy-start.4 = (f32[512,512]{1,0:T(8,128)S(1)}, f32[512,512]{1,0:T(8,128)}, u32[]{:S(2)}) copy-start(f32[512,512]{1,0:T(8,128)} %copy-done.3) | copy-start | bytes 3145732
  (8 other events, 13.0 us)
Sparse Core Ops, SparseCore 0:
  10.1 199.8 all-gather.6
  248.2 68.5 all-gather.10
  320.6 275.4 all-gather.8
where the time goes:
time: 616 us; the launch traced here: 614 us
  waiting for transfers between devices  465 us (75%)
  blocking collectives  42.4 us (7%)
  local copies, waits for them, and re-layouts  34.3 us (6%)
  other arithmetic  27.8 us (5%)
  between operations  24.3 us (4%)
  matrix products  20 us (3%)
    all_gather x2, waiting for transfers between devices, entering(): pieces = jax.tree.map(lambda part: lax.all_gather(part, axis), so_far)  280 us
    all_gather x1, waiting for transfers between devices, sent_together(): filled, at, done = (lax.all_gather(both, axis, axis=dim, tiled=True), 0, [])  185 us
    all_gather x2, blocking collectives, entering(): pieces = jax.tree.map(lambda part: lax.all_gather(part, axis), so_far)  42.4 us
    select_n x2, other arithmetic, accumulate(): jnp.where(latter[0][:, None, None, None] > 0.5, latter[1], earlier[1] + l...  14.3 us
  transfers between devices with their start and end apart: 3, of which 3 were waited for; matrix products, arithmetic and copies ran while one was open for 4% of the time, Pallas kernels for 0%

commit v1 on v0

v1 whole, which is shorter than its diff:
```python
import functools
import math

import jax
import jax.numpy as jnp
from jax import lax
from jax.experimental import pallas as pl
from jax.experimental.pallas import tpu as pltpu
from jax.sharding import PartitionSpec as P

KEY_HEADS = 4
WIDTH = 128
GROUP = 8
ROWS = 128
NZ = 16
HALF = NZ // 2
PARTS = 2
CHUNK = ROWS // PARTS
CHUNKS = KEY_HEADS * 2 * PARTS
SCALE = 1.0 / math.sqrt(WIDTH)
EXP2_SCALE = SCALE * math.log2(math.e)
MASKED = -1e30


def place():
    me = lax.axis_index("ctx")
    return me, me // 2, lax.rem(me, 2)


def depth_of(paths, block):
    total = jnp.int32(-1)
    for e in range(4):
        total = total + (paths[block, e] >= 0).astype(jnp.int32)
    return total


def send(src, dst, send_sem, recv_sem, ctx):
    return pltpu.make_async_remote_copy(
        src_ref=src,
        dst_ref=dst,
        send_sem=send_sem,
        recv_sem=recv_sem,
        device_id={"ctx": ctx},
        device_id_type=pl.DeviceIdType.MESH,
    )


def greet(peers):
    barrier = pltpu.get_barrier_semaphore()
    for peer in peers:
        pl.semaphore_signal(
            barrier, inc=1, device_id={"ctx": peer}, device_id_type=pl.DeviceIdType.MESH
        )
    pl.semaphore_wait(barrier, len(peers))


def spread_kernel(
    paths, keys, values, slots, own, mate, root, seen, out,
    mate_send, mate_recv, root_send, root_recv, root_send2, chain_send, chain_recv,
):
    me, z, y = place()
    up = lax.rem(z + 1, NZ) * 2 + y
    down = lax.rem(z + NZ - 1, NZ) * 2 + y
    partner = z * 2 + 1 - y
    for h in range(KEY_HEADS):
        for t, ref in enumerate((keys, values)):
            first = (h * 2 + t) * PARTS
            own[first : first + PARTS] = ref[:, h * WIDTH : (h + 1) * WIDTH].reshape(
                PARTS, CHUNK, WIDTH
            )
    greet((up, down, partner))

    def to_mate(i):
        return send(own.at[i], mate.at[i], mate_send.at[i], mate_recv.at[i], partner)

    def to_next(i):
        return send(out.at[i], seen.at[i], chain_send.at[i], chain_recv.at[i], up)

    onward = jnp.where(z < HALF, up, down)

    def root_on(i):
        return send(root.at[i], root.at[i], root_send.at[i], root_recv.at[i], onward)

    def root_back(i):
        return send(root.at[i], root.at[i], root_send2.at[i], root_recv.at[i], down)

    @pl.loop(0, CHUNKS)
    def _(i):
        to_mate(i).start()

    d_own = depth_of(paths, me)
    d_mate = depth_of(paths, partner)

    def chain():
        @pl.loop(0, CHUNKS)
        def _(i):
            to_mate(i).wait_recv()
            mine = own[i]
            theirs = mate[i]

            @pl.when(z == 0)
            def _():
                seen[i, 0] = mine
                seen[i, 1] = mine

            @pl.when(z > 0)
            def _():
                to_next(i).wait_recv()

            for e in (1, 2):
                before = seen[i, e - 1]
                mate_hit = d_mate == e
                own_hit = d_own == e
                take_mate = mate_hit & ((y == 0) | (d_own != e))
                out[i, e - 1] = lax.select(
                    take_mate, theirs, lax.select(own_hit, mine, before)
                )
                slots[i, e] = lax.select(mate_hit & (y == 1), theirs, before)

            @pl.when(z < NZ - 1)
            def _():
                to_next(i).start()

    def roots():
        @pl.loop(0, CHUNKS)
        def _(i):
            @pl.when(z == 0)
            def _():
                root[i] = lax.select(y == 0, own[i], mate[i])

            @pl.when(z > 0)
            def _():
                root_on(i).wait_recv()

            slots[i, 0] = root[i]

            @pl.when((z != HALF - 1) & (z != HALF))
            def _():
                root_on(i).start()

            @pl.when(z == 0)
            def _():
                root_back(i).start()

    @pl.when(z >= HALF)
    def _():
        roots()

    chain()

    @pl.when(z < HALF)
    def _():
        roots()

    @pl.loop(0, CHUNKS)
    def _(i):
        to_mate(i).wait_send()

        @pl.when(z < NZ - 1)
        def _():
            to_next(i).wait_send()

        @pl.when((z != HALF - 1) & (z != HALF))
        def _():
            root_on(i).wait_send()

        @pl.when(z == 0)
        def _():
            root_back(i).wait_send()


def attend_kernel(
    paths, assistant, queries, grad_out, keys, values, far, attention, grad_queries, grads,
    bias, live,
):
    me, _, _ = place()
    cols = 2 * ROWS

    @pl.when(pl.program_id(0) == 0)
    def _():
        depth = depth_of(paths, me)
        for e in range(3):
            bias[e * ROWS : (e + 1) * ROWS] = jnp.full(
                (ROWS, cols), jnp.where(e < depth, 0.0, MASKED), jnp.float32
            )
        key_at = lax.broadcasted_iota(jnp.int32, (ROWS, cols), 0)
        row_at = lax.broadcasted_iota(jnp.int32, (ROWS, cols), 1)
        row_at = jnp.where(row_at >= ROWS, row_at - ROWS, row_at)
        bias[3 * ROWS :] = jnp.where(key_at <= row_at, 0.0, MASKED)
        r = lax.broadcasted_iota(jnp.int32, (ROWS, ROWS), 0)
        c = lax.broadcasted_iota(jnp.int32, (ROWS, ROWS), 1)
        spread = jnp.where(r == c, assistant[...].astype(jnp.float32), 0.0)
        live[...] = jnp.broadcast_to(
            jnp.sum(spread, axis=1, keepdims=True), (ROWS, ROWS)
        ).astype(jnp.bfloat16)

    far_keys = [far[0:PARTS, e].reshape(ROWS, WIDTH) for e in range(3)]
    far_values = [far[PARTS : 2 * PARTS, e].reshape(ROWS, WIDTH) for e in range(3)]
    k4 = jnp.concatenate(far_keys + [keys[...]], 0)
    v4 = jnp.concatenate(far_values + [values[...]], 0)
    k4t = k4.T
    v4t = v4.T
    dims = (((1,), (1,)), ((), ()))
    for pair in range(GROUP // 2):
        at = [slice((2 * pair + j) * WIDTH, (2 * pair + j + 1) * WIDTH) for j in range(2)]
        q2 = jnp.concatenate([queries[:, s] for s in at], 0)
        g2 = jnp.concatenate([grad_out[:, s] * live[...] for s in at], 0)
        s = lax.dot_general(k4, q2, dims, preferred_element_type=jnp.float32) + bias[...]
        top = jnp.max(s, axis=0, keepdims=True)
        p = jnp.exp2((s - top) * EXP2_SCALE)
        w = p * (1.0 / jnp.sum(p, axis=0, keepdims=True))
        wb = w.astype(jnp.bfloat16)
        out_t = jnp.dot(v4t, wb, preferred_element_type=jnp.float32)
        dp = lax.dot_general(v4, g2, dims, preferred_element_type=jnp.float32)
        out_t = out_t.astype(jnp.bfloat16)
        delta = jnp.sum(
            g2.T.astype(jnp.float32) * out_t.astype(jnp.float32), axis=0, keepdims=True
        )
        ds = (w * (dp - delta)).astype(jnp.bfloat16)
        gq_t = jnp.dot(k4t, ds, preferred_element_type=jnp.float32) * SCALE
        out = out_t.T
        gq = gq_t.astype(jnp.bfloat16).T
        for j in range(2):
            attention[:, at[j]] = out[j * ROWS : (j + 1) * ROWS]
            grad_queries[:, at[j]] = gq[j * ROWS : (j + 1) * ROWS]
        dk = jnp.dot(ds, q2, preferred_element_type=jnp.float32)
        dv = jnp.dot(wb, g2, preferred_element_type=jnp.float32)
        for t, d in enumerate((dk * SCALE, dv)):
            for e in range(4):
                new = d[e * ROWS : (e + 1) * ROWS].reshape(PARTS, CHUNK, WIDTH)
                here = slice(t * PARTS, (t + 1) * PARTS)
                if pair == 0:
                    grads[here, e] = new
                else:
                    grads[here, e] += new


def gather_kernel(
    paths, grads, grad_keys, grad_values,
    seen, out, total, root_in, root_last, root_out, rooted, to_x, from_x,
    chain_send, chain_recv, root_send, root_recv, last_recv, x_send, x_recv,
):
    me, z, y = place()
    up = lax.rem(z + 1, NZ) * 2 + y
    down = lax.rem(z + NZ - 1, NZ) * 2 + y
    partner = z * 2 + 1 - y
    greet((up, down, partner))
    d0 = depth_of(paths, z * 2)
    d1 = depth_of(paths, z * 2 + 1)
    late = (y == 1).astype(jnp.float32)
    early = 1.0 - late
    hit0 = [(d0 == e).astype(jnp.float32) for e in (1, 2)]
    hit1 = [(d1 == e).astype(jnp.float32) for e in (1, 2)]

    def to_next(i):
        return send(out.at[i], seen.at[i], chain_send.at[i], chain_recv.at[i], down)

    def to_mate(i):
        return send(to_x.at[i], from_x.at[i], x_send.at[i], x_recv.at[i], partner)

    onward = jnp.where(z < HALF, down, up)

    def root_on(i):
        return send(root_out.at[i], root_in.at[i], root_send.at[i], root_recv.at[i], onward)

    def root_end(i):
        return send(root_out.at[i], root_last.at[i], root_send.at[i], last_recv.at[i], onward)

    def chain():
        @pl.loop(0, CHUNKS)
        def _(i):
            @pl.when(z == NZ - 1)
            def _():
                seen[i] = jnp.zeros((2, CHUNK, WIDTH), jnp.bfloat16)

            @pl.when(z < NZ - 1)
            def _():
                to_next(i).wait_recv()

            taken0 = rooted[i]
            taken1 = jnp.zeros((CHUNK, WIDTH), jnp.float32)
            for e in (1, 2):
                before = seen[i, e - 1].astype(jnp.float32)
                mine = grads[i, e]
                taken1 = taken1 + hit1[e - 1] * before
                mid = (1.0 - hit1[e - 1]) * before + late * mine
                taken0 = taken0 + hit0[e - 1] * mid
                out[i, e - 1] = ((1.0 - hit0[e - 1]) * mid + early * mine).astype(jnp.bfloat16)

            @pl.when(z > 0)
            def _():
                to_next(i).start()

            to_x[i] = (early * taken1 + late * taken0).astype(jnp.bfloat16)
            to_mate(i).start()
            total[i] = grads[i, 3] + (early * taken0 + late * taken1)

    def roots():
        @pl.loop(0, CHUNKS)
        def _(i):
            rooted[i] = jnp.zeros((CHUNK, WIDTH), jnp.float32)

            @pl.when((z == HALF - 1) | (z == HALF))
            def _():
                root_out[i] = grads[i, 0].astype(jnp.bfloat16)

            @pl.when((z != HALF - 1) & (z != HALF))
            def _():
                root_on(i).wait_recv()
                root_out[i] = (grads[i, 0] + root_in[i].astype(jnp.float32)).astype(jnp.bfloat16)

            @pl.when(z == 0)
            def _():
                root_end(i).wait_recv()
                rooted[i] = (
                    grads[i, 0]
                    + root_in[i].astype(jnp.float32)
                    + root_last[i].astype(jnp.float32)
                )

            @pl.when((z > 0) & (z < NZ - 1))
            def _():
                root_on(i).start()

            @pl.when(z == NZ - 1)
            def _():
                root_end(i).start()

    @pl.when(z < NZ - 1)
    def _():
        roots()

    @pl.when(z == NZ - 1)
    def _():
        rooted[...] = jnp.zeros_like(rooted)

    chain()

    @pl.when(z == NZ - 1)
    def _():
        roots()

    @pl.loop(0, CHUNKS)
    def _(i):
        to_mate(i).wait_recv()
        total[i] += from_x[i].astype(jnp.float32)

    for h in range(KEY_HEADS):
        for t, ref in enumerate((grad_keys, grad_values)):
            first = (h * 2 + t) * PARTS
            ref[:, h * WIDTH : (h + 1) * WIDTH] = (
                total[first : first + PARTS].reshape(ROWS, WIDTH).astype(jnp.bfloat16)
            )

    @pl.loop(0, CHUNKS)
    def _(i):
        to_mate(i).wait_send()

        @pl.when(z > 0)
        def _():
            to_next(i).wait_send()
            root_on(i).wait_send()


def vmem():
    return pl.BlockSpec(memory_space=pltpu.VMEM)


def smem():
    return pl.BlockSpec(memory_space=pltpu.SMEM)


def on_device(queries, keys, values, grad_out, block_path, assistant):
    sems = pltpu.SemaphoreType.DMA((CHUNKS,))
    one = pltpu.VMEM((CHUNKS, CHUNK, WIDTH), jnp.bfloat16)
    two = pltpu.VMEM((CHUNKS, 2, CHUNK, WIDTH), jnp.bfloat16)
    wide = pltpu.VMEM((CHUNKS, CHUNK, WIDTH), jnp.float32)
    far = pl.pallas_call(
        spread_kernel,
        out_shape=jax.ShapeDtypeStruct((CHUNKS, 3, CHUNK, WIDTH), jnp.bfloat16),
        in_specs=[smem(), vmem(), vmem()],
        out_specs=vmem(),
        scratch_shapes=[one, one, one, two, two] + [sems] * 7,
        compiler_params=pltpu.CompilerParams(collective_id=0, has_side_effects=True),
        name="spread",
    )(block_path, keys, values)

    group = GROUP * WIDTH
    per = 2 * PARTS
    attention, grad_queries, grads = pl.pallas_call(
        attend_kernel,
        grid=(KEY_HEADS,),
        out_shape=(
            jax.ShapeDtypeStruct(queries.shape, jnp.bfloat16),
            jax.ShapeDtypeStruct(queries.shape, jnp.bfloat16),
            jax.ShapeDtypeStruct((CHUNKS, 4, CHUNK, WIDTH), jnp.float32),
        ),
        in_specs=[
            smem(),
            pl.BlockSpec((1, ROWS), lambda g: (0, 0)),
            pl.BlockSpec((ROWS, group), lambda g: (0, g)),
            pl.BlockSpec((ROWS, group), lambda g: (0, g)),
            pl.BlockSpec((ROWS, WIDTH), lambda g: (0, g)),
            pl.BlockSpec((ROWS, WIDTH), lambda g: (0, g)),
            pl.BlockSpec((per, 3, CHUNK, WIDTH), lambda g: (g, 0, 0, 0)),
        ],
        out_specs=(
            pl.BlockSpec((ROWS, group), lambda g: (0, g)),
            pl.BlockSpec((ROWS, group), lambda g: (0, g)),
            pl.BlockSpec((per, 4, CHUNK, WIDTH), lambda g: (g, 0, 0, 0)),
        ),
        scratch_shapes=[
            pltpu.VMEM((4 * ROWS, 2 * ROWS), jnp.float32),
            pltpu.VMEM((ROWS, ROWS), jnp.bfloat16),
        ],
        name="attend",
    )(block_path, assistant.reshape(1, ROWS), queries, grad_out, keys, values, far)

    small = jax.ShapeDtypeStruct(keys.shape, jnp.bfloat16)
    grad_keys, grad_values = pl.pallas_call(
        gather_kernel,
        out_shape=(small, small),
        in_specs=[smem(), vmem()],
        out_specs=(vmem(), vmem()),
        scratch_shapes=[two, two, wide, one, one, one, wide, one, one] + [sems] * 7,
        compiler_params=pltpu.CompilerParams(collective_id=1, has_side_effects=True),
        name="gather",
    )(block_path, grads)
    return attention, grad_queries, grad_keys, grad_values


def solution(mesh):
    rows = P(("leaf", "ctx"), None)
    in_specs = (rows, rows, rows, rows, P("leaf", None), P(("leaf", "ctx")))
    return jax.shard_map(
        on_device, mesh=mesh, in_specs=in_specs, out_specs=(rows,) * 4, check_vma=False
    )
```

time: 616 us -> 157 us (0.25)
  waiting for transfers between devices: 465 us -> 0 us
  Pallas kernels: 0 us -> 152 us
  blocking collectives: 42.4 us -> 0 us
  local copies, waits for them, and re-layouts: 34.3 us -> 4.5 us
  other arithmetic: 27.8 us -> 0 us
  between operations: 24.3 us -> 0.65 us
  matrix products: 20 us -> 0 us
    all_gather x3 -> x0, waiting for transfers between devices: 465 us -> none  [the longest x2 280 us: entering(): pieces = jax.tree.map(lambda part: lax.all_gather(part, axis), so_far)]
    pallas_call x0 -> x3, Pallas kernels: none -> 152 us  [the longest x1 102 us: on_device(): pl.pallas_call(gather_kernel, out_shape=(small, small), in_specs=[smem(),...]
    all_gather x2 -> x0, blocking collectives: 42.4 us -> none  [entering(): pieces = jax.tree.map(lambda part: lax.all_gather(part, axis), so_far)]
    dot_general x24 -> x0, matrix products: 20 us -> none  [the longest x8 6.16 us: dot_cols(): lax.dot_general(left, right, (((0,), (0,)), ((), ())), preferred_element_...]
    select_n x4 -> x0, other arithmetic: 14.3 us -> none  [the longest x2 14.3 us: accumulate(): jnp.where(latter[0][:, None, None, None] > 0.5, latter[1], earlier[1] + l...]
    reshape x18 -> x0, local copies, waits for them, and re-layouts: 13.5 us -> none  [the longest x4 4.56 us: attend_block(): query_matrix = queries[:, key_value_head * head_cols:(key_value_head + 1)...]
    concatenate x6 -> x0, other arithmetic: 8.47 us -> none  [the longest x1 2.3 us: attend_block(): jnp.concatenate(attended_parts, 1)]
    gather x2 -> x0, local copies, waits for them, and re-layouts: 7.2 us -> none  [the longest x1 3.6 us: fill(): value_piece[clipped]]
  transfers between devices with their start and end apart: 3 -> 0, of which waited for: 3 -> 0; matrix products, arithmetic and copies ran while one was open for 4% -> 0% of each run, Pallas kernels for 0% -> 0%
where the time goes in v1:
time: 157 us
  Pallas kernels  152 us (97%)
  local copies, waits for them, and re-layouts  4.5 us (3%)
    pallas_call x1, Pallas kernels, on_device(): pl.pallas_call(gather_kernel, out_shape=(small, small), in_specs=[smem(),...  102 us
    pallas_call x1, Pallas kernels, on_device(): pl.pallas_call(spread_kernel, out_shape=jax.ShapeDtypeStruct((CHUNKS, 3,...  32.4 us
    pallas_call x1, Pallas kernels, on_device(): pl.pallas_call(attend_kernel, grid=(KEY_HEADS,), out_shape=(jax.ShapeDtyp...  17.6 us
    unnamed x3, local copies, waits for them, and re-layouts  4.5 us

profile of v1, /device:TPU:6, one launch (start us, length us, event | category | flops | bytes accessed | tf_op | source)
XLA Modules:
  0.0 156.9 jit_solution(15326853513496091089)
XLA Ops:
  0.6 1.4 copy.11.paths
  2.0 32.4 %spread.1.far = bf16[16,3,64,128]{3,2,1,0:T(8,128)(2,1)} custom-call(s32[32,4]{1,0:T(8,128)} %copy.11.paths, bf16[128,512]{1,0:T(8,128)(2,1)} %keys.3, bf16[128,512]{1,0:T(8,128)(2,1)} %values.3), custom_call_target="tpu_custom_call" | custom-call | tf_op jit(solution)/shard_map/spread/pallas_call | solution.py:378
  34.4 17.6 %attend.1 = (bf16[128,4096]{1,0:T(8,128)(2,1)}, bf16[128,4096]{1,0:T(8,128)(2,1)}, f32[16,4,64,128]{3,2,1,0:T(8,128)}) custom-call(s32[32,4]{1,0:T(8,128)} %copy.11.paths, s32[1,128]{1,0:T(1,128)} %bitcast.1, bf16[128,4096]{1,0:T(8,128)(2,1)} %queries.1, bf16[128,4096]{1,0:T(8,128)(2,1)} %grad_out.1, bf16[128,512]{1,0:T(8,128)(2,1)} %keys.3, ...), custom_call_target="tpu_custom_call" | custom-call | tf_op jit(solution)/shard_map/attend/pallas_call | solution.py:390
  51.9 101.8 %gather.1 = (bf16[128,512]{1,0:T(8,128)(2,1)}, bf16[128,512]{1,0:T(8,128)(2,1)}) custom-call(s32[32,4]{1,0:T(8,128)} %copy.11.paths, f32[16,4,64,128]{3,2,1,0:T(8,128)} %get-tuple-element.11.grads), custom_call_target="tpu_custom_call" | custom-call | tf_op jit(solution)/shard_map/gather/pallas_call | solution.py:420
  153.8 1.6 copy.15
  155.3 1.6 copy.16

commit v2 on v1

--- a/solution.py
+++ b/solution.py
@@ -14,7 +14,7 @@
 ROWS = 128
 NZ = 16
 HALF = NZ // 2
-PARTS = 2
+PARTS = 4
 CHUNK = ROWS // PARTS
 CHUNKS = KEY_HEADS * 2 * PARTS
 SCALE = 1.0 / math.sqrt(WIDTH)

time: 157 us -> 155 us (0.987)
  Pallas kernels: 152 us -> 150 us
    pallas_call x1, Pallas kernels: 102 us -> 99.1 us  [on_device(): pl.pallas_call(gather_kernel, out_shape=(small, small), in_specs=[smem(),...]
where the time goes in v2:
time: 155 us
  Pallas kernels  150 us (97%)
  local copies, waits for them, and re-layouts  4.5 us (3%)
    pallas_call x1, Pallas kernels, on_device(): pl.pallas_call(gather_kernel, out_shape=(small, small), in_specs=[smem(),...  99.1 us
    pallas_call x1, Pallas kernels, on_device(): pl.pallas_call(spread_kernel, out_shape=jax.ShapeDtypeStruct((CHUNKS, 3,...  33.3 us
    pallas_call x1, Pallas kernels, on_device(): pl.pallas_call(attend_kernel, grid=(KEY_HEADS,), out_shape=(jax.ShapeDtyp...  17.6 us
    unnamed x3, local copies, waits for them, and re-layouts  4.5 us

profile of v2, /device:TPU:6, one launch (start us, length us, event | category | flops | bytes accessed | tf_op | source)
XLA Modules:
  0.0 155.0 jit_solution(1736192653934164066)
XLA Ops:
  0.6 1.4 copy.11.paths
  2.0 33.3 %spread.1.far = bf16[32,3,32,128]{3,2,1,0:T(8,128)(2,1)} custom-call(s32[32,4]{1,0:T(8,128)} %copy.11.paths, bf16[128,512]{1,0:T(8,128)(2,1)} %keys.3, bf16[128,512]{1,0:T(8,128)(2,1)} %values.3), custom_call_target="tpu_custom_call" | custom-call | tf_op jit(solution)/shard_map/spread/pallas_call | solution.py:378
  35.3 17.6 %attend.1 = (bf16[128,4096]{1,0:T(8,128)(2,1)}, bf16[128,4096]{1,0:T(8,128)(2,1)}, f32[32,4,32,128]{3,2,1,0:T(8,128)}) custom-call(s32[32,4]{1,0:T(8,128)} %copy.11.paths, s32[1,128]{1,0:T(1,128)} %bitcast.1, bf16[128,4096]{1,0:T(8,128)(2,1)} %queries.1, bf16[128,4096]{1,0:T(8,128)(2,1)} %grad_out.1, bf16[128,512]{1,0:T(8,128)(2,1)} %keys.3, ...), custom_call_target="tpu_custom_call" | custom-call | tf_op jit(solution)/shard_map/attend/pallas_call | solution.py:390
  52.8 99.1 %gather.1 = (bf16[128,512]{1,0:T(8,128)(2,1)}, bf16[128,512]{1,0:T(8,128)(2,1)}) custom-call(s32[32,4]{1,0:T(8,128)} %copy.11.paths, f32[32,4,32,128]{3,2,1,0:T(8,128)} %get-tuple-element.11.grads), custom_call_target="tpu_custom_call" | custom-call | tf_op jit(solution)/shard_map/gather/pallas_call | solution.py:420
  151.9 1.6 %copy.15 = bf16[128,512]{1,0:T(8,128)(2,1)} copy(bf16[128,512]{1,0:T(8,128)(2,1)} %get-tuple-element.20) | data formatting | bytes 262144
  153.5 1.6 %copy.16 = bf16[128,512]{1,0:T(8,128)(2,1)} copy(bf16[128,512]{1,0:T(8,128)(2,1)} %get-tuple-element.21) | data formatting | bytes 262144

commit v3 on v2

--- a/solution.py
+++ b/solution.py
@@ -27,6 +27,11 @@
     return me, me // 2, lax.rem(me, 2)
 
 
+def chip():
+    leaf = lax.axis_index("leaf")
+    return leaf, lax.rem(leaf, 2) == 1
+
+
 def depth_of(paths, block):
     total = jnp.int32(-1)
     for e in range(4):
@@ -34,44 +39,92 @@
     return total
 
 
-def send(src, dst, send_sem, recv_sem, ctx):
+def depth_in(paths, block):
+    at = lax.broadcasted_iota(jnp.int32, paths.shape, 0) == block
+    return jnp.sum((at & (paths >= 0)).astype(jnp.int32)) - 1
+
+
+def send(src, dst, send_sem, recv_sem, ctx, leaf=None):
+    device = {"ctx": ctx} if leaf is None else {"leaf": leaf, "ctx": ctx}
     return pltpu.make_async_remote_copy(
         src_ref=src,
         dst_ref=dst,
         send_sem=send_sem,
         recv_sem=recv_sem,
-        device_id={"ctx": ctx},
+        device_id=device,
         device_id_type=pl.DeviceIdType.MESH,
     )
 
 
 def greet(peers):
     barrier = pltpu.get_barrier_semaphore()
-    for peer in peers:
+    for peer, leaf in peers:
         pl.semaphore_signal(
-            barrier, inc=1, device_id={"ctx": peer}, device_id_type=pl.DeviceIdType.MESH
+            barrier,
+            inc=1,
+            device_id={"leaf": leaf, "ctx": peer},
+            device_id_type=pl.DeviceIdType.MESH,
         )
     pl.semaphore_wait(barrier, len(peers))
 
 
+def meet(leaf, relay, buddy, me, up, down, partner):
+    @pl.when(relay)
+    def _():
+        greet(((up, leaf), (down, leaf), (partner, leaf), (me, buddy), (partner, buddy)))
+
+    @pl.when(jnp.logical_not(relay))
+    def _():
+        greet(((me, buddy), (partner, buddy)))
+
+
 def spread_kernel(
-    paths, keys, values, slots, own, mate, root, seen, out,
-    mate_send, mate_recv, root_send, root_recv, root_send2, chain_send, chain_recv,
+    paths, keys, values, slots, pathv, own, mate, root, seen, out, ready,
+    path_send, path_recv, own_send, own_recv, mate_send, mate_recv,
+    root_send, root_recv, root_send2, chain_send, chain_recv, ready_send, ready_recv,
 ):
     me, z, y = place()
+    leaf, relay = chip()
+    buddy = jnp.where(relay, leaf - 1, leaf + 1)
     up = lax.rem(z + 1, NZ) * 2 + y
     down = lax.rem(z + NZ - 1, NZ) * 2 + y
     partner = z * 2 + 1 - y
-    for h in range(KEY_HEADS):
-        for t, ref in enumerate((keys, values)):
-            first = (h * 2 + t) * PARTS
-            own[first : first + PARTS] = ref[:, h * WIDTH : (h + 1) * WIDTH].reshape(
-                PARTS, CHUNK, WIDTH
-            )
-    greet((up, down, partner))
+
+    def fill(t):
+        for h in range(KEY_HEADS):
+            for k, ref in enumerate((keys, values)):
+                first = (h * 2 + k) * PARTS
+                own[first : first + PARTS, t] = ref[:, h * WIDTH : (h + 1) * WIDTH].reshape(
+                    PARTS, CHUNK, WIDTH
+                )
+        pathv[t] = paths[...]
+
+    @pl.when(relay)
+    def _():
+        fill(1)
+
+    @pl.when(jnp.logical_not(relay))
+    def _():
+        fill(0)
+
+    meet(leaf, relay, buddy, me, up, down, partner)
+
+    def path_over():
+        return send(pathv.at[0], pathv.at[0], path_send, path_recv, me, buddy)
+
+    def own_over(i):
+        return send(own.at[i, 0], own.at[i, 0], own_send.at[i], own_recv.at[i], me, buddy)
+
+    def mate_over(i):
+        return send(
+            own.at[i, 0], mate.at[i, 0], mate_send.at[0, i], mate_recv.at[0, i], partner, buddy
+        )
 
     def to_mate(i):
-        return send(own.at[i], mate.at[i], mate_send.at[i], mate_recv.at[i], partner)
+        return send(own.at[i, 1], mate.at[i, 1], mate_send.at[1, i], mate_recv.at[1, i], partner)
+
+    def hand(i):
+        return send(ready.at[i], slots.at[i], ready_send.at[i], ready_recv.at[i], me, buddy)
 
     def to_next(i):
         return send(out.at[i], seen.at[i], chain_send.at[i], chain_recv.at[i], up)
@@ -84,56 +137,82 @@
     def root_back(i):
         return send(root.at[i], root.at[i], root_send2.at[i], root_recv.at[i], down)
 
-    @pl.loop(0, CHUNKS)
-    def _(i):
-        to_mate(i).start()
-
-    d_own = depth_of(paths, me)
-    d_mate = depth_of(paths, partner)
+    @pl.when(jnp.logical_not(relay))
+    def _():
+        path_over().start()
+
+        @pl.loop(0, CHUNKS)
+        def _(i):
+            own_over(i).start()
+            mate_over(i).start()
+
+        path_over().wait_send()
+
+        @pl.loop(0, CHUNKS)
+        def _(i):
+            hand(i).wait_recv()
+            own_over(i).wait_send()
+            mate_over(i).wait_send()
+
+    roots_first = z > HALF
 
     def chain():
-        @pl.loop(0, CHUNKS)
-        def _(i):
+        path_over().wait_recv()
+        d_own = [depth_in(pathv[t], me) for t in range(2)]
+        d_mate = [depth_in(pathv[t], partner) for t in range(2)]
+
+        @pl.loop(0, CHUNKS)
+        def _(i):
+            own_over(i).wait_recv()
+            mate_over(i).wait_recv()
             to_mate(i).wait_recv()
-            mine = own[i]
-            theirs = mate[i]
 
             @pl.when(z == 0)
             def _():
-                seen[i, 0] = mine
-                seen[i, 1] = mine
+                for t in range(2):
+                    for e in range(2):
+                        seen[i, t, e] = own[i, t]
 
             @pl.when(z > 0)
             def _():
                 to_next(i).wait_recv()
 
-            for e in (1, 2):
-                before = seen[i, e - 1]
-                mate_hit = d_mate == e
-                own_hit = d_own == e
-                take_mate = mate_hit & ((y == 0) | (d_own != e))
-                out[i, e - 1] = lax.select(
-                    take_mate, theirs, lax.select(own_hit, mine, before)
-                )
-                slots[i, e] = lax.select(mate_hit & (y == 1), theirs, before)
+            for t in range(2):
+                mine = own[i, t]
+                theirs = mate[i, t]
+                for e in (1, 2):
+                    before = seen[i, t, e - 1]
+                    take_mate = (d_mate[t] == e) & ((y == 0) | (d_own[t] != e))
+                    out[i, t, e - 1] = lax.select(
+                        take_mate, theirs, lax.select(d_own[t] == e, mine, before)
+                    )
 
             @pl.when(z < NZ - 1)
             def _():
                 to_next(i).start()
 
+            for t, ref in enumerate((ready, slots)):
+                for e in (1, 2):
+                    ref[i, e] = lax.select(
+                        (d_mate[t] == e) & (y == 1), mate[i, t], seen[i, t, e - 1]
+                    )
+
+            @pl.when(roots_first)
+            def _():
+                hand(i).start()
+
     def roots():
         @pl.loop(0, CHUNKS)
         def _(i):
             @pl.when(z == 0)
             def _():
-                root[i] = lax.select(y == 0, own[i], mate[i])
+                for t in range(2):
+                    root[i, t] = lax.select(y == 0, own[i, t], mate[i, t])
 
             @pl.when(z > 0)
             def _():
                 root_on(i).wait_recv()
 
-            slots[i, 0] = root[i]
-
             @pl.when((z != HALF - 1) & (z != HALF))
             def _():
                 root_on(i).start()
@@ -142,31 +221,45 @@
             def _():
                 root_back(i).start()
 
-    @pl.when(z >= HALF)
-    def _():
-        roots()
-
-    chain()
-
-    @pl.when(z < HALF)
-    def _():
-        roots()
-
-    @pl.loop(0, CHUNKS)
-    def _(i):
-        to_mate(i).wait_send()
-
-        @pl.when(z < NZ - 1)
+            ready[i, 0] = root[i, 0]
+            slots[i, 0] = root[i, 1]
+
+            @pl.when(jnp.logical_not(roots_first))
+            def _():
+                hand(i).start()
+
+    @pl.when(relay)
+    def _():
+        @pl.loop(0, CHUNKS)
+        def _(i):
+            to_mate(i).start()
+
+        @pl.when(roots_first)
         def _():
-            to_next(i).wait_send()
-
-        @pl.when((z != HALF - 1) & (z != HALF))
+            roots()
+
+        chain()
+
+        @pl.when(jnp.logical_not(roots_first))
         def _():
-            root_on(i).wait_send()
-
-        @pl.when(z == 0)
-        def _():
-            root_back(i).wait_send()
+            roots()
+
+        @pl.loop(0, CHUNKS)
+        def _(i):
+            to_mate(i).wait_send()
+            hand(i).wait_send()
+
+            @pl.when(z < NZ - 1)
+            def _():
+                to_next(i).wait_send()
+
+            @pl.when((z != HALF - 1) & (z != HALF))
+            def _():
+                root_on(i).wait_send()
+
+            @pl.when(z == 0)
+            def _():
+                root_back(i).wait_send()
 
 
 def attend_kernel(
@@ -237,26 +330,50 @@
 
 def gather_kernel(
     paths, grads, grad_keys, grad_values,
-    seen, out, total, root_in, root_last, root_out, rooted, to_x, from_x,
+    pathv, given, seen, out, total, root_in, root_last, root_out, rooted, to_x, from_x, taken,
+    path_send, path_recv, give_send, give_recv, take_send, take_recv,
     chain_send, chain_recv, root_send, root_recv, last_recv, x_send, x_recv,
 ):
     me, z, y = place()
+    leaf, relay = chip()
+    buddy = jnp.where(relay, leaf - 1, leaf + 1)
     up = lax.rem(z + 1, NZ) * 2 + y
     down = lax.rem(z + NZ - 1, NZ) * 2 + y
     partner = z * 2 + 1 - y
-    greet((up, down, partner))
-    d0 = depth_of(paths, z * 2)
-    d1 = depth_of(paths, z * 2 + 1)
-    late = (y == 1).astype(jnp.float32)
-    early = 1.0 - late
-    hit0 = [(d0 == e).astype(jnp.float32) for e in (1, 2)]
-    hit1 = [(d1 == e).astype(jnp.float32) for e in (1, 2)]
+
+    @pl.when(relay)
+    def _():
+        pathv[1] = paths[...]
+
+    @pl.when(jnp.logical_not(relay))
+    def _():
+        pathv[0] = paths[...]
+
+    meet(leaf, relay, buddy, me, up, down, partner)
+
+    def path_over():
+        return send(pathv.at[0], pathv.at[0], path_send, path_recv, me, buddy)
+
+    def give(i):
+        return send(
+            grads.at[i, pl.ds(0, 3)], given.at[i], give_send.at[i], give_recv.at[i], me, buddy
+        )
+
+    def take(i):
+        return send(taken.at[i], taken.at[i], take_send.at[i], take_recv.at[i], me, buddy)
 
     def to_next(i):
         return send(out.at[i], seen.at[i], chain_send.at[i], chain_recv.at[i], down)
 
     def to_mate(i):
-        return send(to_x.at[i], from_x.at[i], x_send.at[i], x_recv.at[i], partner)
+        return send(
+            to_x.at[i, 1], from_x.at[i], x_send.at[1, i], x_recv.at[i], partner
+        )
+
+    def to_mate_buddy(i):
+        return send(
+            to_x.at[i, 0], from_x.at[i], x_send.at[0, i], x_recv.at[i], partner, buddy
+        )
 
     onward = jnp.where(z < HALF, down, up)
 
@@ -267,56 +384,85 @@
         return send(root_out.at[i], root_last.at[i], root_send.at[i], last_recv.at[i], onward)
 
     def chain():
+        late = (y == 1).astype(jnp.float32)
+        early = 1.0 - late
+        d0 = [depth_in(pathv[t], z * 2) for t in range(2)]
+        d1 = [depth_in(pathv[t], z * 2 + 1) for t in range(2)]
+        hit0 = [[(d0[t] == e).astype(jnp.float32) for e in (1, 2)] for t in range(2)]
+        hit1 = [[(d1[t] == e).astype(jnp.float32) for e in (1, 2)] for t in range(2)]
+
         @pl.loop(0, CHUNKS)
         def _(i):
             @pl.when(z == NZ - 1)
             def _():
-                seen[i] = jnp.zeros((2, CHUNK, WIDTH), jnp.bfloat16)
+                give(i).wait_recv()
+                seen[i] = jnp.zeros((2, 2, CHUNK, WIDTH), jnp.bfloat16)
 
             @pl.when(z < NZ - 1)
             def _():
                 to_next(i).wait_recv()
 
-            taken0 = rooted[i]
-            taken1 = jnp.zeros((CHUNK, WIDTH), jnp.float32)
-            for e in (1, 2):
-                before = seen[i, e - 1].astype(jnp.float32)
-                mine = grads[i, e]
-                taken1 = taken1 + hit1[e - 1] * before
-                mid = (1.0 - hit1[e - 1]) * before + late * mine
-                taken0 = taken0 + hit0[e - 1] * mid
-                out[i, e - 1] = ((1.0 - hit0[e - 1]) * mid + early * mine).astype(jnp.bfloat16)
+            for t, grad in enumerate((given, grads)):
+                for e in (1, 2):
+                    before = seen[i, t, e - 1].astype(jnp.float32)
+                    mine = grad[i, e]
+                    mid = (1.0 - hit1[t][e - 1]) * before + late * mine
+                    out[i, t, e - 1] = (
+                        (1.0 - hit0[t][e - 1]) * mid + early * mine
+                    ).astype(jnp.bfloat16)
 
             @pl.when(z > 0)
             def _():
                 to_next(i).start()
 
-            to_x[i] = (early * taken1 + late * taken0).astype(jnp.bfloat16)
-            to_mate(i).start()
-            total[i] = grads[i, 3] + (early * taken0 + late * taken1)
+            for t, grad in enumerate((given, grads)):
+                taken0 = rooted[i, t]
+                taken1 = jnp.zeros((CHUNK, WIDTH), jnp.float32)
+                for e in (1, 2):
+                    before = seen[i, t, e - 1].astype(jnp.float32)
+                    mid = (1.0 - hit1[t][e - 1]) * before + late * grad[i, e]
+                    taken1 = taken1 + hit1[t][e - 1] * before
+                    taken0 = taken0 + hit0[t][e - 1] * mid
+                to_x[i, t] = (early * taken1 + late * taken0).astype(jnp.bfloat16)
+                if t == 0:
+                    to_mate_buddy(i).start()
+                    taken[i] = early * taken0 + late * taken1
+                    take(i).start()
+                else:
+                    to_mate(i).start()
+                    total[i] = grads[i, 3] + (early * taken0 + late * taken1)
 
     def roots():
         @pl.loop(0, CHUNKS)
         def _(i):
-            rooted[i] = jnp.zeros((CHUNK, WIDTH), jnp.float32)
+            @pl.when(z < NZ - 1)
+            def _():
+                give(i).wait_recv()
+
+            rooted[i] = jnp.zeros((2, CHUNK, WIDTH), jnp.float32)
 
             @pl.when((z == HALF - 1) | (z == HALF))
             def _():
-                root_out[i] = grads[i, 0].astype(jnp.bfloat16)
+                for t, grad in enumerate((given, grads)):
+                    root_out[i, t] = grad[i, 0].astype(jnp.bfloat16)
 
             @pl.when((z != HALF - 1) & (z != HALF))
             def _():
                 root_on(i).wait_recv()
-                root_out[i] = (grads[i, 0] + root_in[i].astype(jnp.float32)).astype(jnp.bfloat16)
+                for t, grad in enumerate((given, grads)):
+                    root_out[i, t] = (
+                        grad[i, 0] + root_in[i, t].astype(jnp.float32)
+                    ).astype(jnp.bfloat16)
 
             @pl.when(z == 0)
             def _():
                 root_end(i).wait_recv()
-                rooted[i] = (
-                    grads[i, 0]
-                    + root_in[i].astype(jnp.float32)
-                    + root_last[i].astype(jnp.float32)
-                )
+                for t, grad in enumerate((given, grads)):
+                    rooted[i, t] = (
+                        grad[i, 0]
+                        + root_in[i, t].astype(jnp.float32)
+                        + root_last[i, t].astype(jnp.float32)
+                    )
 
             @pl.when((z > 0) & (z < NZ - 1))
             def _():
@@ -326,40 +472,65 @@
             def _():
                 root_end(i).start()
 
-    @pl.when(z < NZ - 1)
-    def _():
-        roots()
-
-    @pl.when(z == NZ - 1)
-    def _():
-        rooted[...] = jnp.zeros_like(rooted)
-
-    chain()
-
-    @pl.when(z == NZ - 1)
-    def _():
-        roots()
-
-    @pl.loop(0, CHUNKS)
-    def _(i):
-        to_mate(i).wait_recv()
-        total[i] += from_x[i].astype(jnp.float32)
+    @pl.when(relay)
+    def _():
+        path_over().wait_recv()
+
+        @pl.when(z < NZ - 1)
+        def _():
+            roots()
+
+        @pl.when(z == NZ - 1)
+        def _():
+            rooted[...] = jnp.zeros_like(rooted)
+
+        chain()
+
+        @pl.when(z == NZ - 1)
+        def _():
+            roots()
+
+        @pl.loop(0, CHUNKS)
+        def _(i):
+            to_mate(i).wait_recv()
+            total[i] += from_x[i].astype(jnp.float32)
+
+    @pl.when(jnp.logical_not(relay))
+    def _():
+        path_over().start()
+
+        @pl.loop(0, CHUNKS)
+        def _(i):
+            give(i).start()
+
+        path_over().wait_send()
+
+        @pl.loop(0, CHUNKS)
+        def _(i):
+            take(i).wait_recv()
+            to_mate_buddy(i).wait_recv()
+            total[i] = grads[i, 3] + (taken[i] + from_x[i].astype(jnp.float32))
+            give(i).wait_send()
 
     for h in range(KEY_HEADS):
-        for t, ref in enumerate((grad_keys, grad_values)):
-            first = (h * 2 + t) * PARTS
+        for k, ref in enumerate((grad_keys, grad_values)):
+            first = (h * 2 + k) * PARTS
             ref[:, h * WIDTH : (h + 1) * WIDTH] = (
                 total[first : first + PARTS].reshape(ROWS, WIDTH).astype(jnp.bfloat16)
             )
 
-    @pl.loop(0, CHUNKS)
-    def _(i):
-        to_mate(i).wait_send()
-
-        @pl.when(z > 0)
-        def _():
-            to_next(i).wait_send()
-            root_on(i).wait_send()
+    @pl.when(relay)
+    def _():
+        @pl.loop(0, CHUNKS)
+        def _(i):
+            to_mate(i).wait_send()
+            to_mate_buddy(i).wait_send()
+            take(i).wait_send()
+
+            @pl.when(z > 0)
+            def _():
+                to_next(i).wait_send()
+                root_on(i).wait_send()
 
 
 def vmem():
@@ -371,16 +542,23 @@
 
 
 def on_device(queries, keys, values, grad_out, block_path, assistant):
-    sems = pltpu.SemaphoreType.DMA((CHUNKS,))
-    one = pltpu.VMEM((CHUNKS, CHUNK, WIDTH), jnp.bfloat16)
-    two = pltpu.VMEM((CHUNKS, 2, CHUNK, WIDTH), jnp.bfloat16)
-    wide = pltpu.VMEM((CHUNKS, CHUNK, WIDTH), jnp.float32)
+    sem = pltpu.SemaphoreType.DMA
+    sems = sem((CHUNKS,))
+    both = sem((2, CHUNKS))
+
+    def room(*lead, dtype=jnp.bfloat16):
+        return pltpu.VMEM((CHUNKS, *lead, CHUNK, WIDTH), dtype)
+
+    full = jnp.float32
+    pathv = pltpu.VMEM((2, *block_path.shape), jnp.int32)
     far = pl.pallas_call(
         spread_kernel,
         out_shape=jax.ShapeDtypeStruct((CHUNKS, 3, CHUNK, WIDTH), jnp.bfloat16),
-        in_specs=[smem(), vmem(), vmem()],
+        in_specs=[vmem()] * 3,
         out_specs=vmem(),
-        scratch_shapes=[one, one, one, two, two] + [sems] * 7,
+        scratch_shapes=[pathv, room(2), room(2), room(2), room(2, 2), room(2, 2), room(3)]
+        + [sem, sem, sems, sems, both, both]
+        + [sems] * 7,
         compiler_params=pltpu.CompilerParams(collective_id=0, has_side_effects=True),
         name="spread",
     )(block_path, keys, values)
@@ -420,9 +598,15 @@
     grad_keys, grad_values = pl.pallas_call(
         gather_kernel,
         out_shape=(small, small),
-        in_specs=[smem(), vmem()],
+        in_specs=[vmem()] * 2,
         out_specs=(vmem(), vmem()),
-        scratch_shapes=[two, two, wide, one, one, one, wide, one, one] + [sems] * 7,
+        scratch_shapes=[
+            pathv, room(3, dtype=full), room(2, 2), room(2, 2), room(dtype=full),
+            room(2), room(2), room(2), room(2, dtype=full), room(2), room(), room(dtype=full),
+        ]
+        + [sem, sem]
+        + [sems] * 9
+        + [both, sems],
         compiler_params=pltpu.CompilerParams(collective_id=1, has_side_effects=True),
         name="gather",
     )(block_path, grads)

time: 155 us -> 149 us (0.961); the launches traced: 155 us -> 147 us
  Pallas kernels: 150 us -> 142 us
    pallas_call x1, Pallas kernels: 33.3 us -> 22.3 us  [on_device(): pl.pallas_call(spread_kernel, out_shape=jax.ShapeDtypeStruct((CHUNKS, 3,...]
    pallas_call x1, Pallas kernels: 99.1 us -> 102 us  [on_device(): pl.pallas_call(gather_kernel, out_shape=(small, small), in_specs=[vmem()]...]
where the time goes in v3:
time: 149 us; the launch traced here: 147 us
  Pallas kernels  142 us (95%)
  local copies, waits for them, and re-layouts  4.5 us (3%)
    pallas_call x1, Pallas kernels, on_device(): pl.pallas_call(gather_kernel, out_shape=(small, small), in_specs=[vmem()]...  102 us
    pallas_call x1, Pallas kernels, on_device(): pl.pallas_call(spread_kernel, out_shape=jax.ShapeDtypeStruct((CHUNKS, 3,...  22.3 us
    pallas_call x1, Pallas kernels, on_device(): pl.pallas_call(attend_kernel, grid=(KEY_HEADS,), out_shape=(jax.ShapeDtyp...  17.6 us
    unnamed x3, local copies, waits for them, and re-layouts  4.5 us

profile of v3, /device:TPU:6, one launch (start us, length us, event | category | flops | bytes accessed | tf_op | source)
XLA Modules:
  0.0 147.3 jit_solution(16661474963644790691)
XLA Ops:
  0.6 1.4 copy.11.paths
  2.0 22.3 %spread.1.far = bf16[32,3,32,128]{3,2,1,0:T(8,128)(2,1)} custom-call(s32[32,4]{1,0:T(8,128)} %copy.11.paths, bf16[128,512]{1,0:T(8,128)(2,1)} %keys.3, bf16[128,512]{1,0:T(8,128)(2,1)} %values.3), custom_call_target="tpu_custom_call" | custom-call | tf_op jit(solution)/shard_map/spread/pallas_call | solution.py:554
  24.3 17.6 %attend.1 = (bf16[128,4096]{1,0:T(8,128)(2,1)}, bf16[128,4096]{1,0:T(8,128)(2,1)}, f32[32,4,32,128]{3,2,1,0:T(8,128)}) custom-call(s32[32,4]{1,0:T(8,128)} %copy.11.paths, s32[1,128]{1,0:T(1,128)} %bitcast.1, bf16[128,4096]{1,0:T(8,128)(2,1)} %queries.1, bf16[128,4096]{1,0:T(8,128)(2,1)} %grad_out.1, bf16[128,512]{1,0:T(8,128)(2,1)} %keys.3, ...), custom_call_target="tpu_custom_call" | custom-call | tf_op jit(solution)/shard_map/attend/pallas_call | solution.py:568
  41.9 102.2 %gather.1 = (bf16[128,512]{1,0:T(8,128)(2,1)}, bf16[128,512]{1,0:T(8,128)(2,1)}) custom-call(s32[32,4]{1,0:T(8,128)} %copy.11.paths, f32[32,4,32,128]{3,2,1,0:T(8,128)} %get-tuple-element.11.grads), custom_call_target="tpu_custom_call" | custom-call | tf_op jit(solution)/shard_map/gather/pallas_call | solution.py:598
  144.1 1.6 %copy.15 = bf16[128,512]{1,0:T(8,128)(2,1)} copy(bf16[128,512]{1,0:T(8,128)(2,1)} %get-tuple-element.20) | data formatting | bytes 262144
  145.7 1.6 %copy.16 = bf16[128,512]{1,0:T(8,128)(2,1)} copy(bf16[128,512]{1,0:T(8,128)(2,1)} %get-tuple-element.21) | data formatting | bytes 262144

commit v4 on v0

v4 whole, which is shorter than its diff:
```python
import functools
import math
import types

import jax
import jax.numpy as jnp
from jax import lax
from jax.experimental import pallas as pl
from jax.experimental.pallas import tpu as pltpu
from jax.sharding import PartitionSpec as P

KEY_HEADS = 4
WIDTH = 128
GROUP = 8
ROWS = 128
NZ = 16
UPPER = 10
PARTS = 4
CHUNK = ROWS // PARTS
PER_HEAD = 2 * PARTS
CHUNKS = KEY_HEADS * PER_HEAD
SCALE = 1.0 / math.sqrt(WIDTH)
EXP2_SCALE = SCALE * math.log2(math.e)
MASKED = -1e30


def place():
    me = lax.axis_index("ctx")
    return me, me // 2, lax.rem(me, 2)


def depth_in(paths, block):
    at = lax.broadcasted_iota(jnp.int32, paths.shape, 0) == block
    return jnp.sum((at & (paths >= 0)).astype(jnp.int32)) - 1


def send(src, dst, send_sem, recv_sem, ctx, leaf=None):
    device = {"ctx": ctx} if leaf is None else {"leaf": leaf, "ctx": ctx}
    return pltpu.make_async_remote_copy(
        src_ref=src,
        dst_ref=dst,
        send_sem=send_sem,
        recv_sem=recv_sem,
        device_id=device,
        device_id_type=pl.DeviceIdType.MESH,
    )


def greet(peers):
    barrier = pltpu.get_barrier_semaphore()
    for peer, leaf in peers:
        pl.semaphore_signal(
            barrier,
            inc=1,
            device_id={"leaf": leaf, "ctx": peer},
            device_id_type=pl.DeviceIdType.MESH,
        )
    pl.semaphore_wait(barrier, len(peers))


def scratch(trees):
    def room(*lead, dtype=jnp.bfloat16):
        return pltpu.VMEM((CHUNKS, *lead, CHUNK, WIDTH), dtype)

    full = jnp.float32
    wide = pltpu.VMEM((KEY_HEADS, ROWS, GROUP * WIDTH), jnp.bfloat16)
    sem = pltpu.SemaphoreType.DMA
    one = sem((CHUNKS,))
    two = sem((2, CHUNKS))
    heads = sem((KEY_HEADS,))
    return dict(
        qv=wide, gv=wide, av=wide, zv=wide,
        bias=pltpu.VMEM((4 * ROWS, 2 * ROWS), full),
        live=pltpu.VMEM((ROWS, ROWS), jnp.bfloat16),
        pathv=pltpu.VMEM((2, *trees), jnp.int32),
        own=room(2), mate=room(2), pre=room(2, 2), root=room(2), seen=room(2, 2), out=room(2, 2),
        ready=room(3), slots=room(3),
        grads=room(4, dtype=full), given=room(3, dtype=full), net=room(2, 2), net_in=room(2, 2),
        back=room(2, 2), back_out=room(2, 2), total=room(dtype=full),
        root_in=room(2), root_one=room(2), root_last=room(2), root_out=room(2),
        rooted=room(2, dtype=full), to_x=room(2), from_x=room(), taken=room(dtype=full),
        q_sem=heads, g_sem=heads, a_sem=heads, z_sem=heads,
        path_send=sem, path_recv=sem,
        own_send=one, own_recv=one, mate_send=one, mate_recv=two,
        pre_send=two, pre_recv0=two, pre_recv1=two,
        root_send=one, root_send2=one, root_recv=one,
        chain_send1=one, chain_send2=one, chain_recv=one, hand_send=one, hand_recv=one,
        give_send=one, give_recv=one, take_send=one, take_recv=one,
        net_send=one, net_recv=one, back_send1=one, back_send2=one, back_recv=one,
        sum_send=one, sum_recv=one, sum_recv1=one, sum_recv2=one, x_send=two, x_recv=one,
    )


def attend(h, c, r):
    first = h * PER_HEAD

    def block(at, offset, *where):
        return at[(pl.ds(first + offset, PARTS), *where)].reshape(ROWS, WIDTH)

    k4 = jnp.concatenate([block(r.slots, 0, e) for e in range(3)] + [block(r.own, 0, c)], 0)
    v4 = jnp.concatenate([block(r.slots, PARTS, e) for e in range(3)] + [block(r.own, PARTS, c)], 0)
    k4t = k4.T
    v4t = v4.T
    dims = (((1,), (1,)), ((), ()))
    for pair in range(GROUP // 2):
        at = [slice((2 * pair + j) * WIDTH, (2 * pair + j + 1) * WIDTH) for j in range(2)]
        q2 = jnp.concatenate([r.qv[h, :, s] for s in at], 0)
        g2 = jnp.concatenate([r.gv[h, :, s] * r.live[...] for s in at], 0)
        s = lax.dot_general(k4, q2, dims, preferred_element_type=jnp.float32) + r.bias[...]
        top = jnp.max(s, axis=0, keepdims=True)
        p = jnp.exp2((s - top) * EXP2_SCALE)
        w = p * (1.0 / jnp.sum(p, axis=0, keepdims=True))
        wb = w.astype(jnp.bfloat16)
        out_t = jnp.dot(v4t, wb, preferred_element_type=jnp.float32)
        dp = lax.dot_general(v4, g2, dims, preferred_element_type=jnp.float32)
        out_t = out_t.astype(jnp.bfloat16)
        delta = jnp.sum(
            g2.T.astype(jnp.float32) * out_t.astype(jnp.float32), axis=0, keepdims=True
        )
        ds = (w * (dp - delta)).astype(jnp.bfloat16)
        gq_t = jnp.dot(k4t, ds, preferred_element_type=jnp.float32) * SCALE
        out = out_t.T
        gq = gq_t.astype(jnp.bfloat16).T
        for j in range(2):
            r.av[h, :, at[j]] = out[j * ROWS : (j + 1) * ROWS]
            r.zv[h, :, at[j]] = gq[j * ROWS : (j + 1) * ROWS]
        dk = jnp.dot(ds, q2, preferred_element_type=jnp.float32)
        dv = jnp.dot(wb, g2, preferred_element_type=jnp.float32)
        for t, d in enumerate((dk * SCALE, dv)):
            for e in range(4):
                new = d[e * ROWS : (e + 1) * ROWS].reshape(PARTS, CHUNK, WIDTH)
                here = pl.ds(first + t * PARTS, PARTS)
                if pair == 0:
                    r.grads[here, e] = new
                else:
                    r.grads[here, e] += new


def prepare(depth, assistant, r):
    cols = 2 * ROWS
    for e in range(3):
        r.bias[e * ROWS : (e + 1) * ROWS] = jnp.full(
            (ROWS, cols), jnp.where(e < depth, 0.0, MASKED), jnp.float32
        )
    key_at = lax.broadcasted_iota(jnp.int32, (ROWS, cols), 0)
    row_at = lax.broadcasted_iota(jnp.int32, (ROWS, cols), 1)
    row_at = jnp.where(row_at >= ROWS, row_at - ROWS, row_at)
    r.bias[3 * ROWS :] = jnp.where(key_at <= row_at, 0.0, MASKED)
    i = lax.broadcasted_iota(jnp.int32, (ROWS, ROWS), 0)
    j = lax.broadcasted_iota(jnp.int32, (ROWS, ROWS), 1)
    spread = jnp.where(i == j, assistant[...].astype(jnp.float32), 0.0)
    r.live[...] = jnp.broadcast_to(
        jnp.sum(spread, axis=1, keepdims=True), (ROWS, ROWS)
    ).astype(jnp.bfloat16)


def step_kernel(names, paths, assistant, keys, values, queries, grad_out, *refs):
    attention, grad_queries, grad_keys, grad_values = refs[:4]
    r = types.SimpleNamespace(**dict(zip(names, refs[4:])))
    me, z, y = place()
    leaf = lax.axis_index("leaf")
    c = lax.rem(leaf, 2)
    relay = c == 1
    ends = jnp.logical_not(relay)
    buddy = jnp.where(relay, leaf - 1, leaf + 1)
    odd = lax.rem(z, 2) == 1
    even = jnp.logical_not(odd)
    upper = z >= UPPER
    lower = jnp.logical_not(upper)

    def at(dz, side=None):
        return lax.rem(z + dz + NZ, NZ) * 2 + (y if side is None else side)

    other = 1 - y
    partner = at(0, other)
    pair_z = jnp.where(odd, z - 1, z + 1)

    def column(h):
        return pl.ds(pl.multiple_of(h * GROUP * WIDTH, GROUP * WIDTH), GROUP * WIDTH)

    def q_in(h):
        return pltpu.make_async_copy(queries.at[:, column(h)], r.qv.at[h], r.q_sem.at[h])

    def g_in(h):
        return pltpu.make_async_copy(grad_out.at[:, column(h)], r.gv.at[h], r.g_sem.at[h])

    def a_out(h):
        return pltpu.make_async_copy(r.av.at[h], attention.at[:, column(h)], r.a_sem.at[h])

    def z_out(h):
        return pltpu.make_async_copy(r.zv.at[h], grad_queries.at[:, column(h)], r.z_sem.at[h])

    for h in range(KEY_HEADS):
        q_in(h).start()
        g_in(h).start()
    for h in range(KEY_HEADS):
        for k, ref in enumerate((keys, values)):
            first = (h * 2 + k) * PARTS
            r.own[first : first + PARTS, c] = ref[:, h * WIDTH : (h + 1) * WIDTH].reshape(
                PARTS, CHUNK, WIDTH
            )
    r.pathv[1] = paths[...]

    @pl.when(ends)
    def _():
        r.pathv[0] = paths[...]


    @pl.when(relay)
    def _():
        greet(
            (
                (at(1), leaf), (at(-1), leaf), (at(2), leaf), (at(-2), leaf), (partner, leaf),
                (pair_z * 2 + other, leaf), (me, buddy), (partner, buddy),
                (pair_z * 2 + y, buddy), (pair_z * 2 + other, buddy),
            )
        )

    @pl.when(ends)
    def _():
        greet(
            (
                (me, buddy), (partner, buddy),
                (pair_z * 2 + y, buddy), (pair_z * 2 + other, buddy),
            )
        )

    def path_over():
        return send(r.pathv.at[0], r.pathv.at[0], r.path_send, r.path_recv, me, buddy)

    def own_over(i):
        return send(r.own.at[i, 0], r.own.at[i, 0], r.own_send.at[i], r.own_recv.at[i], me, buddy)

    def to_mate(i, t):
        return send(
            r.own.at[i, t], r.mate.at[i, t], r.mate_send.at[i], r.mate_recv.at[t, i],
            partner, buddy if t == 0 else leaf,
        )

    def to_leader(i, t, j):
        recv = r.pre_recv0 if t == 0 else r.pre_recv1
        return send(
            r.own.at[i, t], r.pre.at[i, t, j], r.pre_send.at[j, i], recv.at[j, i],
            at(1, y if j == 0 else other), buddy if t == 0 else leaf,
        )

    def hand(i):
        return send(r.ready.at[i], r.slots.at[i], r.hand_send.at[i], r.hand_recv.at[i], me, buddy)

    def chain_one(i):
        return send(r.out.at[i], r.seen.at[i], r.chain_send1.at[i], r.chain_recv.at[i], at(1))

    def chain_two(i):
        return send(r.out.at[i], r.seen.at[i], r.chain_send2.at[i], r.chain_recv.at[i], at(2))

    def root_on(i):
        return send(
            r.root.at[i], r.root.at[i], r.root_send.at[i], r.root_recv.at[i],
            jnp.where(lower, at(1), at(-1)),
        )

    def root_back(i):
        return send(r.root.at[i], r.root.at[i], r.root_send2.at[i], r.root_recv.at[i], at(-1))

    def give(i):
        return send(
            r.grads.at[i, pl.ds(0, 3)], r.given.at[i], r.give_send.at[i], r.give_recv.at[i],
            me, buddy,
        )

    def take(i):
        return send(r.taken.at[i], r.taken.at[i], r.take_send.at[i], r.take_recv.at[i], me, buddy)

    def net_over(i):
        return send(r.net.at[i], r.net_in.at[i], r.net_send.at[i], r.net_recv.at[i], at(-1))

    def back_one(i):
        return send(r.back_out.at[i], r.back.at[i], r.back_send1.at[i], r.back_recv.at[i], at(-1))

    def back_two(i):
        return send(r.back_out.at[i], r.back.at[i], r.back_send2.at[i], r.back_recv.at[i], at(-2))

    def sum_on(i):
        return send(
            r.root_out.at[i], r.root_in.at[i], r.sum_send.at[i], r.sum_recv.at[i],
            jnp.where(lower, at(-2), at(1)),
        )

    def sum_one(i):
        return send(r.root_out.at[i], r.root_one.at[i], r.sum_send.at[i], r.sum_recv1.at[i], at(-1))

    def sum_last(i):
        return send(r.root_out.at[i], r.root_last.at[i], r.sum_send.at[i], r.sum_recv2.at[i], at(1))

    def x_over(i, t):
        return send(
            r.to_x.at[i, t], r.from_x.at[i], r.x_send.at[t, i], r.x_recv.at[i],
            partner, buddy if t == 0 else leaf,
        )

    def share(t):
        @pl.loop(0, CHUNKS)
        def _(i):
            to_mate(i, t).start()

            @pl.when(even)
            def _():
                for j in range(2):
                    to_leader(i, t, j).start()

    def shared(t):
        @pl.loop(0, CHUNKS)
        def _(i):
            to_mate(i, t).wait_send()

            @pl.when(even)
            def _():
                for j in range(2):
                    to_leader(i, t, j).wait_send()

    def store_results():
        for h in range(KEY_HEADS):
            for k, ref in enumerate((grad_keys, grad_values)):
                first = (h * 2 + k) * PARTS
                ref[:, h * WIDTH : (h + 1) * WIDTH] = (
                    r.total[first : first + PARTS].reshape(ROWS, WIDTH).astype(jnp.bfloat16)
                )
        for h in range(KEY_HEADS):
            a_out(h).wait()
            z_out(h).wait()

    def compute(h):
        q_in(h).wait()
        g_in(h).wait()
        attend(h, c, r)
        a_out(h).start()
        z_out(h).start()

    @pl.when(ends)
    def _():
        path_over().start()

        @pl.loop(0, CHUNKS)
        def _(i):
            own_over(i).start()

        share(0)

    @pl.when(relay)
    def _():
        share(1)

    prepare(depth_in(paths[...], me), assistant, r)

    @pl.when(relay)
    def _():
        path_over().wait_recv()

    deep = [
        [depth_in(r.pathv[t], b) for b in (z * 2 - 2, z * 2 - 1, z * 2, z * 2 + 1, z * 2 + 2, z * 2 + 3)]
        for t in range(2)
    ]

    def ahead(h):
        @pl.loop(0, PER_HEAD)
        def _(n):
            i = h * PER_HEAD + n
            own_over(i).wait_recv()
            for t in range(2):
                to_mate(i, t).wait_recv()

            @pl.when(z < 2)
            def _():
                for t in range(2):
                    for e in range(2):
                        r.seen[i, t, e] = r.own[i, t]

            @pl.when(odd)
            def _():
                for t in range(2):
                    for j in range(2):
                        to_leader(i, t, j).wait_recv()

            @pl.when(z > 1)
            def _():
                chain_one(i).wait_recv()

            @pl.when(odd)
            def _():
                for t in range(2):
                    d_a, d_b, d_0, d_1 = deep[t][:4]
                    near, far = r.pre[i, t, 0], r.pre[i, t, 1]
                    first = lax.select(y == 0, near, far)
                    second = lax.select(y == 0, far, near)
                    block0 = lax.select(y == 0, r.own[i, t], r.mate[i, t])
                    block1 = lax.select(y == 0, r.mate[i, t], r.own[i, t])
                    for e in (1, 2):
                        mid = lax.select(
                            d_b == e, second, lax.select(d_a == e, first, r.seen[i, t, e - 1])
                        )
                        r.out[i, t, e - 1] = lax.select(
                            d_1 == e, block1, lax.select(d_0 == e, block0, mid)
                        )
                        r.seen[i, t, e - 1] = mid

            @pl.when(odd & (z < NZ - 1))
            def _():
                chain_one(i).start()

            @pl.when(odd & (z < NZ - 2))
            def _():
                chain_two(i).start()

            for t, ref in enumerate((r.ready, r.slots)):
                for e in (1, 2):
                    ref[i, e] = lax.select(
                        (deep[t][2] == e) & (y == 1), r.mate[i, t], r.seen[i, t, e - 1]
                    )

            @pl.when(upper)
            def _():
                hand(i).start()

    def roots():
        @pl.loop(0, CHUNKS)
        def _(i):
            @pl.when(z == 0)
            def _():
                for t in range(2):
                    r.root[i, t] = lax.select(y == 0, r.own[i, t], r.mate[i, t])

            @pl.when(z > 0)
            def _():
                root_on(i).wait_recv()

            @pl.when((z != UPPER - 1) & (z != UPPER))
            def _():
                root_on(i).start()

            @pl.when(z == 0)
            def _():
                root_back(i).start()

            r.ready[i, 0] = r.root[i, 0]
            r.slots[i, 0] = r.root[i, 1]

            @pl.when(lower)
            def _():
                hand(i).start()

    late = (y == 1).astype(jnp.float32)
    early = 1.0 - late

    def keep(t, n):
        return [(deep[t][n] != e).astype(jnp.float32) for e in (1, 2)]

    def nets(h):
        @pl.loop(0, PER_HEAD)
        def _(n):
            i = h * PER_HEAD + n
            give(i).wait_recv()

            @pl.when(odd)
            def _():
                for t, grad in enumerate((r.given, r.grads)):
                    for e in (1, 2):
                        factor = late * keep(t, 2)[e - 1] + early
                        r.net[i, t, e - 1] = (factor * grad[i, e]).astype(jnp.bfloat16)
                net_over(i).start()

    def sums(h):
        @pl.loop(0, PER_HEAD)
        def _(n):
            i = h * PER_HEAD + n
            r.rooted[i] = jnp.zeros((2, CHUNK, WIDTH), jnp.float32)
            starts = (z == UPPER) | (z == UPPER - 1) | (z == UPPER - 2)

            @pl.when(starts)
            def _():
                for t, grad in enumerate((r.given, r.grads)):
                    r.root_out[i, t] = grad[i, 0].astype(jnp.bfloat16)

            @pl.when(jnp.logical_not(starts))
            def _():
                sum_on(i).wait_recv()
                for t, grad in enumerate((r.given, r.grads)):
                    r.root_out[i, t] = (
                        grad[i, 0] + r.root_in[i, t].astype(jnp.float32)
                    ).astype(jnp.bfloat16)

            @pl.when(z == 0)
            def _():
                sum_one(i).wait_recv()
                sum_last(i).wait_recv()
                for t, grad in enumerate((r.given, r.grads)):
                    r.rooted[i, t] = (
                        (grad[i, 0] + r.root_in[i, t].astype(jnp.float32))
                        + (r.root_one[i, t].astype(jnp.float32)
                           + r.root_last[i, t].astype(jnp.float32))
                    )

            @pl.when((z > 1) & (z < NZ - 1))
            def _():
                sum_on(i).start()

            @pl.when(z == 1)
            def _():
                sum_one(i).start()

            @pl.when(z == NZ - 1)
            def _():
                sum_last(i).start()

    def backward(h):
        @pl.loop(0, PER_HEAD)
        def _(n):
            i = h * PER_HEAD + n

            @pl.when(z >= NZ - 2)
            def _():
                r.back[i] = jnp.zeros((2, 2, CHUNK, WIDTH), jnp.bfloat16)

            @pl.when(z < NZ - 2)
            def _():
                back_one(i).wait_recv()

            @pl.when(even)
            def _():
                net_over(i).wait_recv()
                for t, grad in enumerate((r.given, r.grads)):
                    k0, k1, k2, k3 = (keep(t, n) for n in (2, 3, 4, 5))
                    for e in (1, 2):
                        mid = (k2[e - 1] * k3[e - 1]) * r.back[i, t, e - 1].astype(
                            jnp.float32
                        ) + r.net_in[i, t, e - 1].astype(jnp.float32)
                        mine = grad[i, e]
                        after = k1[e - 1] * mid + late * mine
                        r.back_out[i, t, e - 1] = (
                            k0[e - 1] * after + early * mine
                        ).astype(jnp.bfloat16)

            @pl.when(even & (z > 0))
            def _():
                back_one(i).start()
                back_two(i).start()

            use_net = even.astype(jnp.float32)
            for t, grad in enumerate((r.given, r.grads)):
                k0, k1, k2, k3 = (keep(t, n) for n in (2, 3, 4, 5))
                taken0 = r.rooted[i, t]
                taken1 = jnp.zeros((CHUNK, WIDTH), jnp.float32)
                for e in (1, 2):
                    factor = use_net * (k2[e - 1] * k3[e - 1]) + (1.0 - use_net)
                    before = factor * r.back[i, t, e - 1].astype(jnp.float32)
                    before = before + use_net * r.net_in[i, t, e - 1].astype(jnp.float32)
                    taken1 = taken1 + (1.0 - k1[e - 1]) * before
                    after = k1[e - 1] * before + late * grad[i, e]
                    taken0 = taken0 + (1.0 - k0[e - 1]) * after
                r.to_x[i, t] = (early * taken1 + late * taken0).astype(jnp.bfloat16)
                x_over(i, t).start()
                mine = early * taken0 + late * taken1
                if t == 0:
                    r.taken[i] = mine
                    take(i).start()
                else:
                    r.total[i] = r.grads[i, 3] + mine

    @pl.when(odd)
    def _():
        r.net_in[...] = jnp.zeros_like(r.net_in)

    @pl.when(relay)
    def _():
        r.rooted[...] = jnp.zeros_like(r.rooted)

        @pl.when(lower)
        def _():
            @pl.loop(0, KEY_HEADS)
            def _(h):
                ahead(h)

        roots()

    @pl.when(ends)
    def _():
        path_over().wait_send()

    lag = jnp.where(z >= 12, jnp.minimum(NZ - z, 3), KEY_HEADS)

    @pl.loop(0, 2 * KEY_HEADS)
    def _(s):
        @pl.when(relay)
        def _():
            @pl.when(upper & (s < KEY_HEADS))
            def _():
                ahead(s)

            @pl.when((s >= 1) & (s <= KEY_HEADS))
            def _():
                nets(s - 1)

            @pl.when(lower & (s == KEY_HEADS))
            def _():
                @pl.loop(0, KEY_HEADS)
                def _(h):
                    sums(h)

            @pl.when((s >= lag) & (s < lag + KEY_HEADS))
            def _():
                backward(s - lag)

            @pl.when(upper & (s >= 1) & (s <= KEY_HEADS))
            def _():
                sums(s - 1)

        @pl.when(s < KEY_HEADS)
        def _():
            @pl.when(ends)
            def _():
                @pl.loop(0, PER_HEAD)
                def _(n):
                    hand(s * PER_HEAD + n).wait_recv()

            compute(s)

            @pl.when(ends)
            def _():
                @pl.loop(0, PER_HEAD)
                def _(n):
                    give(s * PER_HEAD + n).start()

    @pl.when(relay)
    def _():
        @pl.loop(0, CHUNKS)
        def _(i):
            x_over(i, 1).wait_recv()
            r.total[i] += r.from_x[i].astype(jnp.float32)

    @pl.when(ends)
    def _():
        @pl.loop(0, CHUNKS)
        def _(i):
            take(i).wait_recv()
            x_over(i, 0).wait_recv()
            r.total[i] = r.grads[i, 3] + (r.taken[i] + r.from_x[i].astype(jnp.float32))

    store_results()

    @pl.when(ends)
    def _():
        shared(0)

        @pl.loop(0, CHUNKS)
        def _(i):
            own_over(i).wait_send()
            give(i).wait_send()

    @pl.when(relay)
    def _():
        shared(1)

        @pl.loop(0, CHUNKS)
        def _(i):
            hand(i).wait_send()
            take(i).wait_send()
            for t in range(2):
                x_over(i, t).wait_send()

            @pl.when((z != UPPER - 1) & (z != UPPER))
            def _():
                root_on(i).wait_send()

            @pl.when(z == 0)
            def _():
                root_back(i).wait_send()

            @pl.when(z > 0)
            def _():
                sum_on(i).wait_send()

            @pl.when(odd & (z < NZ - 1))
            def _():
                chain_one(i).wait_send()

            @pl.when(odd & (z < NZ - 2))
            def _():
                chain_two(i).wait_send()

            @pl.when(odd)
            def _():
                net_over(i).wait_send()

            @pl.when(even & (z > 0))
            def _():
                back_one(i).wait_send()
                back_two(i).wait_send()


def on_device(queries, keys, values, grad_out, block_path, assistant):
    extra = scratch(block_path.shape)
    vmem = pl.BlockSpec(memory_space=pltpu.VMEM)
    anywhere = pl.BlockSpec(memory_space=pl.ANY)
    wide = jax.ShapeDtypeStruct(queries.shape, jnp.bfloat16)
    small = jax.ShapeDtypeStruct(keys.shape, jnp.bfloat16)
    return pl.pallas_call(
        functools.partial(step_kernel, tuple(extra)),
        out_shape=(wide, wide, small, small),
        in_specs=[vmem] * 4 + [anywhere] * 2,
        out_specs=(anywhere, anywhere, vmem, vmem),
        scratch_shapes=list(extra.values()),
        compiler_params=pltpu.CompilerParams(collective_id=0, has_side_effects=True),
        name="step",
    )(block_path, assistant.reshape(1, ROWS), keys, values, queries, grad_out)


def solution(mesh):
    rows = P(("leaf", "ctx"), None)
    in_specs = (rows, rows, rows, rows, P("leaf", None), P(("leaf", "ctx")))
    return jax.shard_map(
        on_device, mesh=mesh, in_specs=in_specs, out_specs=(rows,) * 4, check_vma=False
    )
```

time: 616 us -> 140 us (0.23)
  waiting for transfers between devices: 465 us -> 0 us
  Pallas kernels: 0 us -> 132 us
  blocking collectives: 42.4 us -> 0 us
  local copies, waits for them, and re-layouts: 34.3 us -> 6.37 us
  other arithmetic: 27.8 us -> 0 us
  between operations: 24.3 us -> 0.65 us
  matrix products: 20 us -> 0 us
    all_gather x3 -> x0, waiting for transfers between devices: 465 us -> none  [the longest x2 280 us: entering(): pieces = jax.tree.map(lambda part: lax.all_gather(part, axis), so_far)]
    pallas_call x0 -> x1, Pallas kernels: none -> 132 us  [on_device(): pl.pallas_call(functools.partial(step_kernel, tuple(extra)), out_shape=(w...]
    all_gather x2 -> x0, blocking collectives: 42.4 us -> none  [entering(): pieces = jax.tree.map(lambda part: lax.all_gather(part, axis), so_far)]
    dot_general x24 -> x0, matrix products: 20 us -> none  [the longest x8 6.16 us: dot_cols(): lax.dot_general(left, right, (((0,), (0,)), ((), ())), preferred_element_...]
    select_n x4 -> x0, other arithmetic: 14.3 us -> none  [the longest x2 14.3 us: accumulate(): jnp.where(latter[0][:, None, None, None] > 0.5, latter[1], earlier[1] + l...]
    reshape x18 -> x0, local copies, waits for them, and re-layouts: 13.5 us -> none  [the longest x4 4.56 us: attend_block(): query_matrix = queries[:, key_value_head * head_cols:(key_value_head + 1)...]
    concatenate x6 -> x0, other arithmetic: 8.47 us -> none  [the longest x1 2.3 us: attend_block(): jnp.concatenate(attended_parts, 1)]
    gather x2 -> x0, local copies, waits for them, and re-layouts: 7.2 us -> none  [the longest x1 3.6 us: fill(): value_piece[clipped]]
  transfers between devices with their start and end apart: 3 -> 0, of which waited for: 3 -> 0; matrix products, arithmetic and copies ran while one was open for 4% -> 0% of each run, Pallas kernels for 0% -> 0%
where the time goes in v4:
time: 140 us; the launch traced here: 139 us
  Pallas kernels  132 us (94%)
  local copies, waits for them, and re-layouts  6.37 us (5%)
    pallas_call x1, Pallas kernels, on_device(): pl.pallas_call(functools.partial(step_kernel, tuple(extra)), out_shape=(w...  132 us
    unnamed x11, local copies, waits for them, and re-layouts  6.37 us

profile of v4, /device:TPU:6, one launch (start us, length us, event | category | flops | bytes accessed | tf_op | source)
XLA Modules:
  0.0 138.6 jit_solution(109056691653024836)
XLA Ops:
  0.6 1.4 copy.10.paths
  2.0 131.5 %step.1 = (bf16[128,4096]{1,0:T(8,128)(2,1)}, bf16[128,4096]{1,0:T(8,128)(2,1)}, bf16[128,512]{1,0:T(8,128)(2,1)}, bf16[128,512]{1,0:T(8,128)(2,1)}) custom-call(s32[32,4]{1,0:T(8,128)} %copy.10.paths, s32[1,128]{1,0:T(1,128)} %bitcast.1, bf16[128,512]{1,0:T(8,128)(2,1)} %keys.1, bf16[128,512]{1,0:T(8,128)(2,1)} %values.1, bf16[128,4096]{1,0:T(8,128)(2,1)} %queries.1, ...), custom_call_target="tpu_custom_call" | custom-call | tf_op jit(solution)/shard_map/step/pallas_call | solution.py:705
  133.5 0.0 copy-start
  133.5 2.4 %copy.15 = bf16[128,4096]{1,0:T(8,128)(2,1)} copy(bf16[128,4096]{1,0:T(8,128)(2,1)} %get-tuple-element.8) | data formatting | bytes 2097152
  135.9 0.0 copy-done
  135.9 0.0 copy-start.2
  135.9 1.0 copy.16
  136.9 0.1 copy-done.2
  136.9 0.0 copy-start.1
  137.0 0.7 copy.17
  137.6 0.3 copy-done.1
  137.9 0.7 copy.18
Async XLA Ops:
  133.5 2.4 %copy-start = (bf16[128,4096]{1,0:T(8,128)(2,1)S(1)}, bf16[128,4096]{1,0:T(8,128)(2,1)}, u32[]{:S(2)}) copy-start(bf16[128,4096]{1,0:T(8,128)(2,1)} %get-tuple-element.9) | copy-start | bytes 3145732
  135.9 1.0 copy-start.2
  136.9 1.0 copy-start.1

commit v5 on v4

v5 whole, which is shorter than its diff:
```python
import functools
import math
import types

import jax
import jax.numpy as jnp
from jax import lax
from jax.experimental import pallas as pl
from jax.experimental.pallas import tpu as pltpu
from jax.sharding import PartitionSpec as P

KEY_HEADS = 4
WIDTH = 128
GROUP = 8
ROWS = 128
NZ = 16
UPPER = 10
ROOT_UP = 5
PARTS = 2
CHUNK = ROWS // PARTS
PER_HEAD = 2 * PARTS
CHUNKS = KEY_HEADS * PER_HEAD
SCALE = 1.0 / math.sqrt(WIDTH)
EXP2_SCALE = SCALE * math.log2(math.e)
MASKED = -1e30


def place():
    me = lax.axis_index("ctx")
    return me, me // 2, lax.rem(me, 2)


def depth_in(paths, block):
    at = lax.broadcasted_iota(jnp.int32, paths.shape, 1) == block
    return jnp.sum((at & (paths >= 0)).astype(jnp.int32)) - 1


def send(src, dst, send_sem, recv_sem, ctx, leaf=None):
    device = {"ctx": ctx} if leaf is None else {"leaf": leaf, "ctx": ctx}
    return pltpu.make_async_remote_copy(
        src_ref=src,
        dst_ref=dst,
        send_sem=send_sem,
        recv_sem=recv_sem,
        device_id=device,
        device_id_type=pl.DeviceIdType.MESH,
    )


def greet(peers):
    barrier = pltpu.get_barrier_semaphore()
    for peer, leaf in peers:
        pl.semaphore_signal(
            barrier,
            inc=1,
            device_id={"leaf": leaf, "ctx": peer},
            device_id_type=pl.DeviceIdType.MESH,
        )
    pl.semaphore_wait(barrier, len(peers))


def scratch(trees):
    def room(*lead, dtype=jnp.bfloat16):
        return pltpu.VMEM((CHUNKS, *lead, CHUNK, WIDTH), dtype)

    full = jnp.float32
    wide = pltpu.VMEM((KEY_HEADS, ROWS, GROUP * WIDTH), jnp.bfloat16)
    sem = pltpu.SemaphoreType.DMA
    one = sem((CHUNKS,))
    two = sem((2, CHUNKS))
    heads = sem((KEY_HEADS,))
    return dict(
        qv=wide, gv=wide, av=wide, zv=wide,
        bias=pltpu.VMEM((4 * ROWS, 2 * ROWS), full),
        live=pltpu.VMEM((ROWS, ROWS), jnp.bfloat16),
        pathv=pltpu.VMEM((2, *trees), jnp.int32),
        own=room(2), mate=room(2), pair=room(2), pre=room(2), root=room(2),
        seen=room(2), out=room(2), base=room(2), side=room(2),
        ready=room(2), slots=room(3),
        grads=room(4, dtype=full), given=room(3, dtype=full), swap=room(2), swap_in=room(2),
        net=room(2), net_in=room(2), back=room(2), back_out=room(2), total=room(dtype=full),
        root_in=room(2), root_last=room(2), root_out=room(2),
        rooted=room(2, dtype=full), ra=room(dtype=full), rb=room(dtype=full), zero=room(dtype=full), to_x=room(2), from_x=room(), taken=room(dtype=full),
        q_sem=heads, g_sem=heads, a_sem=heads, z_sem=heads,
        path_send=sem, path_recv=sem,
        own_send=one, own_recv=one, mate_send=one, mate_recv=two,
        pre_send=one, pre_recv=one, side_send=one, side_recv=one, swap_send=one, swap_recv=one,
        root_send=one, root_send1=one, root_send2=one, root_send3=one, over_send=one, over_recv=one,
        zero_send=one, zero_recv=one, ra_send=one, ra_recv=one, rb_send=two, rb_recv=one, root_recv=one,
        chain_send1=one, chain_send2=one, chain_recv=one, hand_send=one, hand_recv=one,
        give_send=one, give_recv=one, take_send=one, take_recv=one,
        net_send=one, net_recv=one, back_send1=one, back_send2=one, back_recv=one,
        sum_send=one, sum_recv=one, sum_recv2=one, x_send=two, x_recv=one,
    )


def attend(h, c, r):
    first = h * PER_HEAD

    def block(at, offset, *where):
        return at[(pl.ds(first + offset, PARTS), *where)].reshape(ROWS, WIDTH)

    k4 = jnp.concatenate([block(r.slots, 0, e) for e in range(3)] + [block(r.own, 0, c)], 0)
    v4 = jnp.concatenate([block(r.slots, PARTS, e) for e in range(3)] + [block(r.own, PARTS, c)], 0)
    k4t = k4.T
    v4t = v4.T
    dims = (((1,), (1,)), ((), ()))
    for pair in range(GROUP // 2):
        at = [slice((2 * pair + j) * WIDTH, (2 * pair + j + 1) * WIDTH) for j in range(2)]
        q2 = jnp.concatenate([r.qv[h, :, s] for s in at], 0)
        g2 = jnp.concatenate([r.gv[h, :, s] * r.live[...] for s in at], 0)
        s = lax.dot_general(k4, q2, dims, preferred_element_type=jnp.float32) + r.bias[...]
        top = jnp.max(s, axis=0, keepdims=True)
        p = jnp.exp2((s - top) * EXP2_SCALE)
        w = p * (1.0 / jnp.sum(p, axis=0, keepdims=True))
        wb = w.astype(jnp.bfloat16)
        out_t = jnp.dot(v4t, wb, preferred_element_type=jnp.float32)
        dp = lax.dot_general(v4, g2, dims, preferred_element_type=jnp.float32)
        out_t = out_t.astype(jnp.bfloat16)
        delta = jnp.sum(
            g2.T.astype(jnp.float32) * out_t.astype(jnp.float32), axis=0, keepdims=True
        )
        ds = (w * (dp - delta)).astype(jnp.bfloat16)
        gq_t = jnp.dot(k4t, ds, preferred_element_type=jnp.float32) * SCALE
        out = out_t.T
        gq = gq_t.astype(jnp.bfloat16).T
        for j in range(2):
            r.av[h, :, at[j]] = out[j * ROWS : (j + 1) * ROWS]
            r.zv[h, :, at[j]] = gq[j * ROWS : (j + 1) * ROWS]
        dk = jnp.dot(ds, q2, preferred_element_type=jnp.float32)
        dv = jnp.dot(wb, g2, preferred_element_type=jnp.float32)
        for t, d in enumerate((dk * SCALE, dv)):
            for e in range(4):
                new = d[e * ROWS : (e + 1) * ROWS].reshape(PARTS, CHUNK, WIDTH)
                here = pl.ds(first + t * PARTS, PARTS)
                if pair == 0:
                    r.grads[here, e] = new
                else:
                    r.grads[here, e] += new


def prepare(depth, assistant, r):
    cols = 2 * ROWS
    for e in range(3):
        r.bias[e * ROWS : (e + 1) * ROWS] = jnp.full(
            (ROWS, cols), jnp.where(e < depth, 0.0, MASKED), jnp.float32
        )
    key_at = lax.broadcasted_iota(jnp.int32, (ROWS, cols), 0)
    row_at = lax.broadcasted_iota(jnp.int32, (ROWS, cols), 1)
    row_at = jnp.where(row_at >= ROWS, row_at - ROWS, row_at)
    r.bias[3 * ROWS :] = jnp.where(key_at <= row_at, 0.0, MASKED)
    i = lax.broadcasted_iota(jnp.int32, (ROWS, ROWS), 0)
    j = lax.broadcasted_iota(jnp.int32, (ROWS, ROWS), 1)
    spread = jnp.where(i == j, assistant[...].astype(jnp.float32), 0.0)
    r.live[...] = jnp.broadcast_to(
        jnp.sum(spread, axis=1, keepdims=True), (ROWS, ROWS)
    ).astype(jnp.bfloat16)


def step_kernel(names, paths, assistant, keys, values, queries, grad_out, *refs):
    attention, grad_queries, grad_keys, grad_values = refs[:4]
    r = types.SimpleNamespace(**dict(zip(names, refs[4:])))
    me, z, y = place()
    leaf = lax.axis_index("leaf")
    c = lax.rem(leaf, 2)
    relay = c == 1
    ends = jnp.logical_not(relay)
    buddy = jnp.where(relay, leaf - 1, leaf + 1)
    odd = lax.rem(z, 2) == 1
    even = jnp.logical_not(odd)
    upper = z >= UPPER
    lower = jnp.logical_not(upper)

    def at(dz, side=None):
        return lax.rem(z + dz + NZ, NZ) * 2 + (y if side is None else side)

    other = 1 - y
    partner = at(0, other)
    lane = 1 + y
    far_lane = 2 - y

    def column(h):
        return pl.ds(pl.multiple_of(h * GROUP * WIDTH, GROUP * WIDTH), GROUP * WIDTH)

    def q_in(h):
        return pltpu.make_async_copy(queries.at[:, column(h)], r.qv.at[h], r.q_sem.at[h])

    def g_in(h):
        return pltpu.make_async_copy(grad_out.at[:, column(h)], r.gv.at[h], r.g_sem.at[h])

    def a_out(h):
        return pltpu.make_async_copy(r.av.at[h], attention.at[:, column(h)], r.a_sem.at[h])

    def z_out(h):
        return pltpu.make_async_copy(r.zv.at[h], grad_queries.at[:, column(h)], r.z_sem.at[h])

    for h in range(KEY_HEADS):
        q_in(h).start()
        g_in(h).start()
    for h in range(KEY_HEADS):
        for k, ref in enumerate((keys, values)):
            first = (h * 2 + k) * PARTS
            r.own[first : first + PARTS, c] = ref[:, h * WIDTH : (h + 1) * WIDTH].reshape(
                PARTS, CHUNK, WIDTH
            )
    r.pathv[1] = paths[...]

    @pl.when(ends)
    def _():
        r.pathv[0] = paths[...]


    greet(
        (
            (at(1), leaf), (at(-1), leaf), (at(2), leaf), (at(-2), leaf), (partner, leaf),
            (me, buddy), (partner, buddy), (at(1), buddy), (at(-1), buddy),
            (at(2), buddy), (at(-2), buddy),
        )
    )

    def path_over():
        return send(r.pathv.at[0], r.pathv.at[0], r.path_send, r.path_recv, me, buddy)

    def own_over(i):
        return send(r.own.at[i, 0], r.own.at[i, 0], r.own_send.at[i], r.own_recv.at[i], me, buddy)

    def to_mate(i, t):
        return send(
            r.own.at[i, t], r.mate.at[i, t], r.mate_send.at[i], r.mate_recv.at[t, i],
            partner, buddy if t == 0 else leaf,
        )

    def to_leader(i):
        return send(r.pair.at[i], r.pre.at[i], r.pre_send.at[i], r.pre_recv.at[i], at(1))

    def side_over(i):
        return send(r.base.at[i], r.side.at[i], r.side_send.at[i], r.side_recv.at[i], partner)

    def swap_over(i):
        return send(r.swap.at[i], r.swap_in.at[i], r.swap_send.at[i], r.swap_recv.at[i], partner)

    def hand(i):
        return send(
            r.ready.at[i], r.slots.at[i, pl.ds(1, 2)], r.hand_send.at[i], r.hand_recv.at[i],
            me, buddy,
        )

    def chain_one(i):
        return send(r.out.at[i], r.seen.at[i], r.chain_send1.at[i], r.chain_recv.at[i], at(1))

    def chain_two(i):
        return send(r.out.at[i], r.seen.at[i], r.chain_send2.at[i], r.chain_recv.at[i], at(2))

    def root_to(i, dz, sem, side):
        return send(r.root.at[i], r.root.at[i], sem.at[i], r.root_recv.at[i], at(dz), side)

    root_dz = jnp.where(z <= ROOT_UP, 1, -2)
    root_more = (z > ROOT_UP + 2) | ((z > 0) & (z < ROOT_UP))

    def root_on(i):
        return root_to(i, root_dz, r.root_send, leaf)

    def root_low(i):
        return root_to(i, 1, r.root_send, buddy)

    def root_high(i, dz):
        return root_to(i, dz, r.root_send1 if dz == -1 else r.root_send2, buddy)

    def root_stay(i):
        return send(r.root.at[i], r.root.at[i], r.root_send3.at[i], r.root_recv.at[i], me, buddy)

    def root_over(i):
        return send(
            r.root.at[i, 1], r.slots.at[i, 0], r.over_send.at[i], r.over_recv.at[i], me, buddy
        )

    def give(i):
        return send(
            r.grads.at[i, pl.ds(0, 3)], r.given.at[i], r.give_send.at[i], r.give_recv.at[i],
            me, buddy,
        )

    def take(i):
        return send(r.taken.at[i], r.taken.at[i], r.take_send.at[i], r.take_recv.at[i], me, buddy)

    def net_over(i):
        return send(r.net.at[i], r.net_in.at[i], r.net_send.at[i], r.net_recv.at[i], at(-1))

    def back_one(i):
        return send(r.back_out.at[i], r.back.at[i], r.back_send1.at[i], r.back_recv.at[i], at(-1))

    def back_two(i):
        return send(r.back_out.at[i], r.back.at[i], r.back_send2.at[i], r.back_recv.at[i], at(-2))

    def zero_over(i):
        return send(
            r.grads.at[i, 0], r.zero.at[i], r.zero_send.at[i], r.zero_recv.at[i], me, buddy
        )

    def sum_on(i):
        return send(r.root_out.at[i], r.root_in.at[i], r.sum_send.at[i], r.sum_recv.at[i], at(2))

    def sum_last(i):
        return send(r.root_out.at[i], r.root_last.at[i], r.sum_send.at[i], r.sum_recv2.at[i], at(1))

    def sum_home(i):
        return send(r.rooted.at[i, 1], r.ra.at[i], r.ra_send.at[i], r.ra_recv.at[i], me, buddy)

    def sum_mate(i, t):
        return send(
            r.rooted.at[i, t], r.rb.at[i], r.rb_send.at[t, i], r.rb_recv.at[i],
            partner, leaf if t == 0 else buddy,
        )

    def x_over(i, t):
        return send(
            r.to_x.at[i, t], r.from_x.at[i], r.x_send.at[t, i], r.x_recv.at[i],
            partner, buddy if t == 0 else leaf,
        )

    def share(t):
        @pl.loop(0, CHUNKS)
        def _(i):
            to_mate(i, t).start()

    def store_results():
        for h in range(KEY_HEADS):
            for k, ref in enumerate((grad_keys, grad_values)):
                first = (h * 2 + k) * PARTS
                ref[:, h * WIDTH : (h + 1) * WIDTH] = (
                    r.total[first : first + PARTS].reshape(ROWS, WIDTH).astype(jnp.bfloat16)
                )
        for h in range(KEY_HEADS):
            a_out(h).wait()
            z_out(h).wait()

    def compute(h):
        q_in(h).wait()
        g_in(h).wait()
        attend(h, c, r)
        a_out(h).start()
        z_out(h).start()

    @pl.when(ends)
    def _():
        path_over().start()

        @pl.loop(0, CHUNKS)
        def _(i):
            own_over(i).start()

        share(0)

    @pl.when(relay)
    def _():
        share(1)

    prepare(depth_in(paths[...], me), assistant, r)

    @pl.when(relay)
    def _():
        path_over().wait_recv()

    deep = [
        [depth_in(r.pathv[t], b) for b in (z * 2 - 2, z * 2 - 1, z * 2, z * 2 + 1, z * 2 + 2, z * 2 + 3)]
        for t in range(2)
    ]

    def first_last(i, t):
        mine, theirs = r.own[i, t], r.mate[i, t]
        return lax.select(y == 0, mine, theirs), lax.select(y == 0, theirs, mine)

    def pairs(h):
        @pl.loop(0, PER_HEAD)
        def _(n):
            i = h * PER_HEAD + n
            own_over(i).wait_recv()
            for t in range(2):
                to_mate(i, t).wait_recv()

            @pl.when(even)
            def _():
                for t in range(2):
                    block0, block1 = first_last(i, t)
                    r.pair[i, t] = lax.select(deep[t][3] == lane, block1, block0)
                to_leader(i).start()

            @pl.when(z < 2)
            def _():
                r.seen[i] = r.own[i]

            @pl.when(z == 0)
            def _():
                for t in range(2):
                    r.root[i, t] = first_last(i, t)[0]
                for dz in (-1, -2):
                    root_high(i, dz).start()

    def ahead(h):
        @pl.loop(0, PER_HEAD)
        def _(n):
            i = h * PER_HEAD + n

            @pl.when(odd)
            def _():
                to_leader(i).wait_recv()

            @pl.when(z > 1)
            def _():
                chain_one(i).wait_recv()

            @pl.when(odd)
            def _():
                for t in range(2):
                    d_a, d_b, d_0, d_1 = deep[t][:4]
                    block0, block1 = first_last(i, t)
                    mid = lax.select((d_a == lane) | (d_b == lane), r.pre[i, t], r.seen[i, t])
                    r.out[i, t] = lax.select(
                        d_1 == lane, block1, lax.select(d_0 == lane, block0, mid)
                    )
                    r.base[i, t] = mid

            @pl.when(odd & (z < NZ - 2))
            def _():
                chain_two(i).start()

            @pl.when(odd & (z < NZ - 1))
            def _():
                chain_one(i).start()

            @pl.when(even)
            def _():
                r.base[i] = r.seen[i]

            side_over(i).start()

    def place_slots(h):
        @pl.loop(0, PER_HEAD)
        def _(n):
            i = h * PER_HEAD + n
            side_over(i).wait_recv()
            for t, ref, shift in ((0, r.ready, 1), (1, r.slots, 0)):
                for slot, at_z in ((lane, r.base), (far_lane, r.side)):
                    ref[i, slot - shift] = lax.select(
                        (deep[t][2] == slot) & (y == 1), r.mate[i, t], at_z[i, t]
                    )
            hand(i).start()

    def roots():
        @pl.loop(0, CHUNKS)
        def _(i):
            root_on(i).wait_recv()

            @pl.when(root_more)
            def _():
                root_on(i).start()

            root_over(i).start()
            r.slots[i, 0] = r.root[i, 0]

    late = (y == 1).astype(jnp.float32)
    early = 1.0 - late

    def keep(t, n):
        return (deep[t][n] != lane).astype(jnp.float32)

    def both_grads(i, t):
        mine = (r.given, r.grads)[t][i, lane]
        theirs = r.swap_in[i, t].astype(jnp.float32)
        return early * mine + late * theirs, late * mine + early * theirs

    def swaps(h):
        @pl.loop(0, PER_HEAD)
        def _(n):
            i = h * PER_HEAD + n
            give(i).wait_recv()
            for t, grad in enumerate((r.given, r.grads)):
                r.swap[i, t] = grad[i, far_lane].astype(jnp.bfloat16)
            swap_over(i).start()

    def nets(h):
        @pl.loop(0, PER_HEAD)
        def _(n):
            i = h * PER_HEAD + n
            swap_over(i).wait_recv()

            @pl.when(odd)
            def _():
                for t in range(2):
                    g0, g1 = both_grads(i, t)
                    r.net[i, t] = (keep(t, 2) * g1 + g0).astype(jnp.bfloat16)
                net_over(i).start()

    def sums():
        starts = (z == 1) | (z == 2)

        @pl.loop(0, CHUNKS)
        def _(i):
            zero_over(i).wait_recv()
            mine = (r.grads[i, 0], r.zero[i])

            @pl.when(starts)
            def _():
                for t in range(2):
                    r.root_out[i, t] = mine[t].astype(jnp.bfloat16)

            @pl.when(jnp.logical_not(starts))
            def _():
                sum_on(i).wait_recv()

            @pl.when(z > 2)
            def _():
                for t in range(2):
                    r.root_out[i, t] = (
                        mine[t] + r.root_in[i, t].astype(jnp.float32)
                    ).astype(jnp.bfloat16)

            @pl.when((z > 0) & (z < NZ - 1))
            def _():
                sum_on(i).start()

            @pl.when(z == NZ - 1)
            def _():
                sum_last(i).start()

            @pl.when(z == 0)
            def _():
                sum_last(i).wait_recv()
                for t in range(2):
                    r.rooted[i, t] = (
                        mine[t]
                        + r.root_in[i, t].astype(jnp.float32)
                        + r.root_last[i, t].astype(jnp.float32)
                    )

            @pl.when(me == 0)
            def _():
                sum_home(i).start()

            @pl.when(me == 1)
            def _():
                for t in range(2):
                    sum_mate(i, t).start()

    def backward(h):
        @pl.loop(0, PER_HEAD)
        def _(n):
            i = h * PER_HEAD + n

            @pl.when(z >= NZ - 2)
            def _():
                r.back[i] = jnp.zeros((2, CHUNK, WIDTH), jnp.bfloat16)

            @pl.when(z < NZ - 2)
            def _():
                back_one(i).wait_recv()

            @pl.when(even)
            def _():
                net_over(i).wait_recv()

            use_net = even.astype(jnp.float32)
            kept = []
            for t in range(2):
                k0, k1 = keep(t, 2), keep(t, 3)
                g0, g1 = both_grads(i, t)
                factor = use_net * (keep(t, 4) * keep(t, 5)) + (1.0 - use_net)
                before = factor * r.back[i, t].astype(jnp.float32)
                before = before + r.net_in[i, t].astype(jnp.float32)
                after = k1 * before + g1
                r.back_out[i, t] = (k0 * after + g0).astype(jnp.bfloat16)
                kept.append(((1.0 - k0) * after, (1.0 - k1) * before))

            @pl.when(even & (z > 0))
            def _():
                back_two(i).start()
                back_one(i).start()

            for t in range(2):
                taken0, taken1 = kept[t]
                r.to_x[i, t] = (early * taken1 + late * taken0).astype(jnp.bfloat16)
                x_over(i, t).start()
                mine = early * taken0 + late * taken1
                if t == 0:
                    r.taken[i] = mine
                    take(i).start()
                else:
                    r.total[i] = r.grads[i, 3] + mine

    @pl.when(odd)
    def _():
        r.net_in[...] = jnp.zeros_like(r.net_in)

    @pl.when(relay)
    def _():
        @pl.when(z > 1)
        def _():
            @pl.loop(0, KEY_HEADS)
            def _(h):
                pairs(h)

        @pl.when(lower)
        def _():
            @pl.loop(0, KEY_HEADS)
            def _(h):
                @pl.when(z < 2)
                def _():
                    pairs(h)

                ahead(h)

        @pl.when(z == 0)
        def _():
            @pl.loop(0, CHUNKS)
            def _(i):
                root_low(i).start()
                root_stay(i).start()
                r.slots[i, 0] = r.root[i, 1]

        @pl.when(lower)
        def _():
            @pl.loop(0, KEY_HEADS)
            def _(h):
                place_slots(h)

        @pl.when(upper)
        def _():
            ahead(0)

    @pl.when(ends)
    def _():
        path_over().wait_send()

        @pl.when(z > 0)
        def _():
            roots()

        @pl.when(z == 0)
        def _():
            @pl.loop(0, CHUNKS)
            def _(i):
                root_on(i).wait_recv()
                r.slots[i, 0] = r.root[i, 0]

    lag = jnp.where(z >= 12, jnp.minimum(NZ - z, 3), KEY_HEADS)

    @pl.loop(0, 2 * KEY_HEADS)
    def _(s):
        @pl.when(relay)
        def _():
            @pl.when((s >= 1) & (s <= KEY_HEADS))
            def _():
                swaps(s - 1)

            @pl.when(upper & (s < KEY_HEADS - 1))
            def _():
                ahead(s + 1)

            @pl.when(upper & (s < KEY_HEADS))
            def _():
                place_slots(s)

            @pl.when((s >= 1) & (s <= KEY_HEADS))
            def _():
                nets(s - 1)

            @pl.when((s >= lag) & (s < lag + KEY_HEADS))
            def _():
                backward(s - lag)

        @pl.when(s < KEY_HEADS)
        def _():
            @pl.when(ends)
            def _():
                @pl.loop(0, PER_HEAD)
                def _(n):
                    hand(s * PER_HEAD + n).wait_recv()

            @pl.when(relay & (z > 0))
            def _():
                @pl.loop(0, PER_HEAD)
                def _(n):
                    root_over(s * PER_HEAD + n).wait_recv()

            compute(s)

            @pl.when(relay)
            def _():
                @pl.loop(0, PER_HEAD)
                def _(n):
                    zero_over(s * PER_HEAD + n).start()

            @pl.when(ends)
            def _():
                @pl.loop(0, PER_HEAD)
                def _(n):
                    give(s * PER_HEAD + n).start()

    @pl.when(relay)
    def _():
        @pl.loop(0, CHUNKS)
        def _(i):
            x_over(i, 1).wait_recv()
            r.total[i] += r.from_x[i].astype(jnp.float32)

            @pl.when(me == 0)
            def _():
                sum_home(i).wait_recv()
                sum_mate(i, 1).wait_recv()
                r.total[i] += r.ra[i] + r.rb[i]

    @pl.when(ends)
    def _():
        sums()

        @pl.loop(0, CHUNKS)
        def _(i):
            take(i).wait_recv()
            x_over(i, 0).wait_recv()
            r.total[i] = r.grads[i, 3] + (r.taken[i] + r.from_x[i].astype(jnp.float32))

            @pl.when(me == 0)
            def _():
                sum_mate(i, 0).wait_recv()
                r.total[i] += r.rooted[i, 0] + r.rb[i]

    store_results()

    @pl.when(ends)
    def _():
        @pl.loop(0, CHUNKS)
        def _(i):
            to_mate(i, 0).wait_send()
            own_over(i).wait_send()
            give(i).wait_send()

            @pl.when(z > 0)
            def _():
                root_over(i).wait_send()
                sum_on(i).wait_send()

            @pl.when(root_more)
            def _():
                root_on(i).wait_send()

            @pl.when(me == 0)
            def _():
                sum_home(i).wait_send()

            @pl.when(me == 1)
            def _():
                for t in range(2):
                    sum_mate(i, t).wait_send()

    @pl.when(relay)
    def _():
        @pl.loop(0, CHUNKS)
        def _(i):
            to_mate(i, 1).wait_send()
            side_over(i).wait_send()
            swap_over(i).wait_send()
            hand(i).wait_send()
            take(i).wait_send()
            for t in range(2):
                x_over(i, t).wait_send()

            zero_over(i).wait_send()

            @pl.when(z == 0)
            def _():
                root_low(i).wait_send()
                root_stay(i).wait_send()
                for dz in (-1, -2):
                    root_high(i, dz).wait_send()

            @pl.when(even)
            def _():
                to_leader(i).wait_send()

            @pl.when(odd & (z < NZ - 1))
            def _():
                chain_one(i).wait_send()

            @pl.when(odd & (z < NZ - 2))
            def _():
                chain_two(i).wait_send()

            @pl.when(odd)
            def _():
                net_over(i).wait_send()

            @pl.when(even & (z > 0))
            def _():
                back_one(i).wait_send()
                back_two(i).wait_send()


def on_device(queries, keys, values, grad_out, block_path, assistant):
    paths = block_path.T
    extra = scratch(paths.shape)
    vmem = pl.BlockSpec(memory_space=pltpu.VMEM)
    anywhere = pl.BlockSpec(memory_space=pl.ANY)
    wide = jax.ShapeDtypeStruct(queries.shape, jnp.bfloat16)
    small = jax.ShapeDtypeStruct(keys.shape, jnp.bfloat16)
    return pl.pallas_call(
        functools.partial(step_kernel, tuple(extra)),
        out_shape=(wide, wide, small, small),
        in_specs=[vmem] * 4 + [anywhere] * 2,
        out_specs=(anywhere, anywhere, vmem, vmem),
        scratch_shapes=list(extra.values()),
        compiler_params=pltpu.CompilerParams(collective_id=0, has_side_effects=True),
        name="step",
    )(paths, assistant.reshape(1, ROWS), keys, values, queries, grad_out)


def solution(mesh):
    rows = P(("leaf", "ctx"), None)
    in_specs = (rows, rows, rows, rows, P("leaf", None), P(("leaf", "ctx")))
    return jax.shard_map(
        on_device, mesh=mesh, in_specs=in_specs, out_specs=(rows,) * 4, check_vma=False
    )
```

time: 140 us -> 122 us (0.87)
  Pallas kernels: 132 us -> 114 us
    pallas_call x1, Pallas kernels: 132 us -> 114 us  [on_device(): pl.pallas_call(functools.partial(step_kernel, tuple(extra)), out_shape=(w...]
    unnamed x11 -> x10, local copies, waits for them, and re-layouts: 6.37 us -> 5.01 us
where the time goes in v5:
time: 122 us; the launch traced here: 120 us
  Pallas kernels  114 us (93%)
  local copies, waits for them, and re-layouts  5.01 us (4%)
    pallas_call x1, Pallas kernels, on_device(): pl.pallas_call(functools.partial(step_kernel, tuple(extra)), out_shape=(w...  114 us
    unnamed x10, local copies, waits for them, and re-layouts  5.01 us

profile of v5, /device:TPU:6, one launch (start us, length us, event | category | flops | bytes accessed | tf_op | source)
XLA Modules:
  0.0 120.2 jit_solution(12795370855216285210)
XLA Ops:
  0.6 114.5 %step.1 = (bf16[128,4096]{1,0:T(8,128)(2,1)}, bf16[128,4096]{1,0:T(8,128)(2,1)}, bf16[128,512]{1,0:T(8,128)(2,1)}, bf16[128,512]{1,0:T(8,128)(2,1)}) custom-call(s32[4,32]{1,0:T(4,128)} %bitcast.2, s32[1,128]{1,0:T(1,128)} %bitcast.3, bf16[128,512]{1,0:T(8,128)(2,1)} %keys.1, bf16[128,512]{1,0:T(8,128)(2,1)} %values.1, bf16[128,4096]{1,0:T(8,128)(2,1)} %queries.1, ...), custom_call_target="tpu_custom_call" | custom-call | tf_op jit(solution)/shard_map/step/pallas_call | solution.py:805
  115.1 0.0 copy-start
  115.1 2.4 %copy.14 = bf16[128,4096]{1,0:T(8,128)(2,1)} copy(bf16[128,4096]{1,0:T(8,128)(2,1)} %get-tuple-element.8) | data formatting | bytes 2097152
  117.5 0.0 copy-done
  117.5 0.0 copy-start.2
  117.5 1.0 copy.15
  118.5 0.1 copy-done.2
  118.5 0.0 copy-start.1
  118.5 0.7 copy.16
  119.2 0.3 copy-done.1
  119.5 0.7 copy.17
Async XLA Ops:
  115.1 2.4 %copy-start = (bf16[128,4096]{1,0:T(8,128)(2,1)S(1)}, bf16[128,4096]{1,0:T(8,128)(2,1)}, u32[]{:S(2)}) copy-start(bf16[128,4096]{1,0:T(8,128)(2,1)} %get-tuple-element.9) | copy-start | bytes 3145732
  117.5 1.0 copy-start.2
  118.5 1.0 copy-start.1

commit v6 on v5

--- a/solution.py
+++ b/solution.py
@@ -15,8 +15,10 @@
 ROWS = 128
 NZ = 16
 UPPER = 10
-ROOT_UP = 5
+ROOT_UP = 4
+SUM_DOWN = 7
 PARTS = 2
+CUTS = 4
 CHUNK = ROWS // PARTS
 PER_HEAD = 2 * PARTS
 CHUNKS = KEY_HEADS * PER_HEAD
@@ -73,13 +75,17 @@
         qv=wide, gv=wide, av=wide, zv=wide,
         bias=pltpu.VMEM((4 * ROWS, 2 * ROWS), full),
         live=pltpu.VMEM((ROWS, ROWS), jnp.bfloat16),
+        d_all=pltpu.VMEM((4 * ROWS, GROUP * ROWS), jnp.bfloat16),
+        w_all=pltpu.VMEM((4 * ROWS, GROUP * ROWS), jnp.bfloat16),
+        q_all=pltpu.VMEM((GROUP * ROWS, WIDTH), jnp.bfloat16),
+        g_all=pltpu.VMEM((GROUP * ROWS, WIDTH), jnp.bfloat16),
         pathv=pltpu.VMEM((2, *trees), jnp.int32),
         own=room(2), mate=room(2), pair=room(2), pre=room(2), root=room(2),
         seen=room(2), out=room(2), base=room(2), side=room(2),
         ready=room(2), slots=room(3),
         grads=room(4, dtype=full), given=room(3, dtype=full), swap=room(2), swap_in=room(2),
         net=room(2), net_in=room(2), back=room(2), back_out=room(2), total=room(dtype=full),
-        root_in=room(2), root_last=room(2), root_out=room(2),
+        root_in=room(2), root_end=room(2), root_last=room(2), root_out=room(2),
         rooted=room(2, dtype=full), ra=room(dtype=full), rb=room(dtype=full), zero=room(dtype=full), to_x=room(2), from_x=room(), taken=room(dtype=full),
         q_sem=heads, g_sem=heads, a_sem=heads, z_sem=heads,
         path_send=sem, path_recv=sem,
@@ -90,7 +96,7 @@
         chain_send1=one, chain_send2=one, chain_recv=one, hand_send=one, hand_recv=one,
         give_send=one, give_recv=one, take_send=one, take_recv=one,
         net_send=one, net_recv=one, back_send1=one, back_send2=one, back_recv=one,
-        sum_send=one, sum_recv=one, sum_recv2=one, x_send=two, x_recv=one,
+        sum_send=one, sum_recv=one, sum_recv1=one, sum_recv2=one, x_send=two, x_recv=one,
     )
 
 
@@ -127,16 +133,18 @@
         for j in range(2):
             r.av[h, :, at[j]] = out[j * ROWS : (j + 1) * ROWS]
             r.zv[h, :, at[j]] = gq[j * ROWS : (j + 1) * ROWS]
-        dk = jnp.dot(ds, q2, preferred_element_type=jnp.float32)
-        dv = jnp.dot(wb, g2, preferred_element_type=jnp.float32)
-        for t, d in enumerate((dk * SCALE, dv)):
-            for e in range(4):
-                new = d[e * ROWS : (e + 1) * ROWS].reshape(PARTS, CHUNK, WIDTH)
-                here = pl.ds(first + t * PARTS, PARTS)
-                if pair == 0:
-                    r.grads[here, e] = new
-                else:
-                    r.grads[here, e] += new
+        here = slice(pair * 2 * ROWS, (pair + 1) * 2 * ROWS)
+        r.d_all[:, here] = ds
+        r.w_all[:, here] = wb
+        r.q_all[here] = q2
+        r.g_all[here] = g2
+    dk = jnp.dot(r.d_all[...], r.q_all[...], preferred_element_type=jnp.float32) * SCALE
+    dv = jnp.dot(r.w_all[...], r.g_all[...], preferred_element_type=jnp.float32)
+    for t, d in enumerate((dk, dv)):
+        for e in range(4):
+            r.grads[pl.ds(first + t * PARTS, PARTS), e] = d[
+                e * ROWS : (e + 1) * ROWS
+            ].reshape(PARTS, CHUNK, WIDTH)
 
 
 def prepare(depth, assistant, r):
@@ -298,7 +306,13 @@
         )
 
     def sum_on(i):
-        return send(r.root_out.at[i], r.root_in.at[i], r.sum_send.at[i], r.sum_recv.at[i], at(2))
+        return send(
+            r.root_out.at[i], r.root_in.at[i], r.sum_send.at[i], r.sum_recv.at[i],
+            at(jnp.where(z <= SUM_DOWN, -1, 2)),
+        )
+
+    def sum_end(i):
+        return send(r.root_out.at[i], r.root_end.at[i], r.sum_send.at[i], r.sum_recv1.at[i], at(2))
 
     def sum_last(i):
         return send(r.root_out.at[i], r.root_last.at[i], r.sum_send.at[i], r.sum_recv2.at[i], at(1))
@@ -492,7 +506,7 @@
                 net_over(i).start()
 
     def sums():
-        starts = (z == 1) | (z == 2)
+        starts = (z == SUM_DOWN) | (z == SUM_DOWN + 1) | (z == SUM_DOWN + 2)
 
         @pl.loop(0, CHUNKS)
         def _(i):
@@ -508,28 +522,32 @@
             def _():
                 sum_on(i).wait_recv()
 
-            @pl.when(z > 2)
+            @pl.when(jnp.logical_not(starts) & (z > 0))
             def _():
                 for t in range(2):
                     r.root_out[i, t] = (
                         mine[t] + r.root_in[i, t].astype(jnp.float32)
                     ).astype(jnp.bfloat16)
 
-            @pl.when((z > 0) & (z < NZ - 1))
+            @pl.when((z > 0) & (z < NZ - 2))
             def _():
                 sum_on(i).start()
 
+            @pl.when(z == NZ - 2)
+            def _():
+                sum_end(i).start()
+
             @pl.when(z == NZ - 1)
             def _():
                 sum_last(i).start()
 
             @pl.when(z == 0)
             def _():
+                sum_end(i).wait_recv()
                 sum_last(i).wait_recv()
                 for t in range(2):
-                    r.rooted[i, t] = (
-                        mine[t]
-                        + r.root_in[i, t].astype(jnp.float32)
+                    r.rooted[i, t] = (mine[t] + r.root_in[i, t].astype(jnp.float32)) + (
+                        r.root_end[i, t].astype(jnp.float32)
                         + r.root_last[i, t].astype(jnp.float32)
                     )
 
@@ -795,6 +813,32 @@
                 back_two(i).wait_send()
 
 
+def finish_kernel(cuts, *refs):
+    sources, results, held = refs[:4], refs[4:8], refs[8:12]
+    in_sem, out_sem = refs[12:]
+
+    def rows(j, cut):
+        size = ROWS // (CUTS if j < 2 else 1)
+        return pl.ds(cut * size, size)
+
+    loads, stores = [], []
+    for n, (j, cut) in enumerate(cuts):
+        at = rows(j, cut)
+        loads.append(
+            pltpu.make_async_copy(sources[j].at[at], held[j].at[at], in_sem.at[n])
+        )
+        stores.append(
+            pltpu.make_async_copy(held[j].at[at], results[j].at[at], out_sem.at[n])
+        )
+    for load in loads:
+        load.start()
+    for load, store in zip(loads, stores):
+        load.wait()
+        store.start()
+    for store in stores:
+        store.wait()
+
+
 def on_device(queries, keys, values, grad_out, block_path, assistant):
     paths = block_path.T
     extra = scratch(paths.shape)
@@ -802,7 +846,7 @@
     anywhere = pl.BlockSpec(memory_space=pl.ANY)
     wide = jax.ShapeDtypeStruct(queries.shape, jnp.bfloat16)
     small = jax.ShapeDtypeStruct(keys.shape, jnp.bfloat16)
-    return pl.pallas_call(
+    results = pl.pallas_call(
         functools.partial(step_kernel, tuple(extra)),
         out_shape=(wide, wide, small, small),
         in_specs=[vmem] * 4 + [anywhere] * 2,
@@ -811,6 +855,16 @@
         compiler_params=pltpu.CompilerParams(collective_id=0, has_side_effects=True),
         name="step",
     )(paths, assistant.reshape(1, ROWS), keys, values, queries, grad_out)
+    cuts = [(j, cut) for j in range(2) for cut in range(CUTS)] + [(2, 0), (3, 0)]
+    return pl.pallas_call(
+        functools.partial(finish_kernel, cuts),
+        out_shape=(wide, wide, small, small),
+        in_specs=[anywhere] * 4,
+        out_specs=(anywhere,) * 4,
+        scratch_shapes=[pltpu.VMEM(a.shape, a.dtype) for a in (wide, wide, small, small)]
+        + [pltpu.SemaphoreType.DMA((len(cuts),))] * 2,
+        name="finish",
+    )(*results)
 
 
 def solution(mesh):

time: 122 us -> 114 us (0.934)
  local copies, waits for them, and re-layouts: 5.01 us -> 0 us
  Pallas kernels: 114 us -> 112 us
    pallas_call x1, Pallas kernels: 114 us -> 109 us  [on_device(): pl.pallas_call(functools.partial(step_kernel, tuple(extra)), out_shape=(w...]
    unnamed x10 -> x0, local copies, waits for them, and re-layouts: 5.01 us -> none
    pallas_call x0 -> x1, Pallas kernels: none -> 2.51 us  [on_device(): pl.pallas_call(functools.partial(finish_kernel, cuts), out_shape=(wide, w...]
where the time goes in v6:
time: 114 us; the launch traced here: 112 us
  Pallas kernels  112 us (98%)
    pallas_call x1, Pallas kernels, on_device(): pl.pallas_call(functools.partial(step_kernel, tuple(extra)), out_shape=(w...  109 us
    pallas_call x1, Pallas kernels, on_device(): pl.pallas_call(functools.partial(finish_kernel, cuts), out_shape=(wide, w...  2.51 us

profile of v6, /device:TPU:6, one launch (start us, length us, event | category | flops | bytes accessed | tf_op | source)
XLA Modules:
  0.0 112.4 jit_solution(7524828004732068186)
XLA Ops:
  0.6 109.3 %step.1 = (bf16[128,4096]{1,0:T(8,128)(2,1)}, bf16[128,4096]{1,0:T(8,128)(2,1)}, bf16[128,512]{1,0:T(8,128)(2,1)}, bf16[128,512]{1,0:T(8,128)(2,1)}) custom-call(s32[4,32]{1,0:T(4,128)} %bitcast.2, s32[1,128]{1,0:T(1,128)} %bitcast.3, bf16[128,512]{1,0:T(8,128)(2,1)} %keys.1, bf16[128,512]{1,0:T(8,128)(2,1)} %values.1, bf16[128,4096]{1,0:T(8,128)(2,1)} %queries.1, ...), custom_call_target="tpu_custom_call" | custom-call | tf_op jit(solution)/shard_map/step/pallas_call | solution.py:849
  109.9 2.5 %finish.1 = (bf16[128,4096]{1,0:T(8,128)(2,1)}, bf16[128,4096]{1,0:T(8,128)(2,1)}, bf16[128,512]{1,0:T(8,128)(2,1)}, bf16[128,512]{1,0:T(8,128)(2,1)}) custom-call(bf16[128,4096]{1,0:T(8,128)(2,1)} %get-tuple-element.8.refs_0_, bf16[128,4096]{1,0:T(8,128)(2,1)} %get-tuple-element.9.refs_1_, bf16[128,512]{1,0:T(8,128)(2,1)} %get-tuple-element.10.refs_2_, ...), custom_call_target="tpu_custom_call" | custom-call | tf_op jit(solution)/shard_map/finish/pallas_call | solution.py:859
